TPU v7x, 256 devices: a whole 4x4x8 slice. The times are simulated.
256 devices in a mesh: outer: 8 (over y, core), inner: 32 (over x, z).
Axes of the slice: x: 4, y: 4, z: 8, core: 2. Of those that a mesh axis runs over, the one named last changes fastest.
Arguments:
- amplitudes: float32 [2, 67108864], P(None, ('outer', 'inner')), may hold values from -200 to 200
Outputs:
- transformed: float32 [2, 67108864], P(None, ('outer', 'inner'))
- checks: float32 [3], replicated
All inputs are finite; a program needn't handle non-finite values.
Results may differ from a plain program's by a relative error of at most 0.00007.
Values sent between devices are 32-bit elements; how exact they have to be, the bound alone decides.
A program may use at most 64 MiB of HBM per device.

v0:
```python
import math

import jax
import jax.numpy as jnp
from jax import lax
from jax.sharding import Mesh
from jax.sharding import PartitionSpec as P

WINDOW = 9
OUTER = ("outer_0", "outer_1")
INNER = ("inner_0", "inner_1")
OUTER_INNER = ("outer_0", "outer_1", "inner_0", "inner_1")


def one_axis_at_a_time(value, axes):
    for axis in axes:
        value = lax.psum(value, axis)
    return value


def cut_along(value, dim, peers):
    before, after = (value.shape[:dim], value.shape[dim + 1 :])
    return jnp.moveaxis(value.reshape(*before, peers, -1, *after), dim, 0)


def in_order(parts, dim):
    lengths = list(parts.shape[1:])
    lengths[dim] *= parts.shape[0]
    return jnp.moveaxis(parts, 0, dim).reshape(lengths)


def exchange_both(value, axis, axes, splits, concats):
    sizes = [lax.axis_size(a) for a in axes]
    parts = cut_along(value, splits[0], sizes[0])
    parts = jnp.moveaxis(cut_along(parts, splits[1] + 1, sizes[1]), 0, 1)
    inside = parts.shape[2:]
    parts = parts.reshape(-1, *inside)
    parts = lax.all_to_all(parts, axis, split_axis=0, concat_axis=0, tiled=True)
    parts = in_order(parts.reshape(*sizes, *inside), concats[0] + 1)
    return in_order(parts, concats[1])


def reverse_index(values, count):
    result = jnp.zeros_like(values)
    for bit_pos in range(count):
        result = result | (values >> bit_pos & 1) << count - 1 - bit_pos
    return result


def reversal_table(size, count):
    indices = jnp.arange(size, dtype=jnp.int32)
    return (reverse_index(indices, count)[:, None] == indices[None, :]).astype(jnp.float32)


def check_terms(current, positions, angle_scale):
    angles = positions.astype(jnp.float32) * angle_scale
    cosine = jnp.cos(angles)
    sine = jnp.sin(angles)
    squares = jnp.sum(current * current)
    phase_real = jnp.sum(current[0] * cosine + current[1] * sine)
    phase_imag = jnp.sum(current[1] * cosine - current[0] * sine)
    return (squares, phase_real, phase_imag)


def per_device(amplitudes):
    amp_dev = amplitudes.shape[1]
    n_outer = lax.axis_size(OUTER)
    n_inner = lax.axis_size(INNER)
    outer_bits = n_outer.bit_length() - 1
    inner_bits = n_inner.bit_length() - 1
    global_bits = outer_bits + inner_bits
    local_bits = amp_dev.bit_length() - 1
    n_devices = n_outer * n_inner
    high_count = amp_dev // n_devices
    total_len = amp_dev * n_devices
    columns = 2**WINDOW
    rows_count = amp_dev // columns
    column_ids = jnp.arange(columns, dtype=jnp.int32)
    reversed_ids = reverse_index(column_ids, WINDOW)
    products = column_ids[:, None] * reversed_ids[None, :] % columns
    angles = products.astype(jnp.float32) * (2.0 * math.pi / columns)
    real_part = jnp.cos(angles) / math.sqrt(columns)
    imag_part = jnp.sin(angles) / math.sqrt(columns)
    table = jnp.concatenate(
        [jnp.concatenate([real_part, imag_part], 1), jnp.concatenate([-imag_part, real_part], 1)], 0
    )
    stacked = jnp.concatenate(
        [amplitudes[0].reshape(rows_count, columns), amplitudes[1].reshape(rows_count, columns)], 1
    )
    result = jnp.dot(
        stacked, table, precision=lax.Precision.HIGHEST, preferred_element_type=jnp.float32
    )
    windowed = jnp.stack([result[:, :columns].reshape(-1), result[:, columns:].reshape(-1)])
    device_id = lax.axis_index(OUTER) * n_inner + lax.axis_index(INNER)
    angle_scale = 2.0 * math.pi / total_len
    local_ids = jnp.arange(amp_dev, dtype=jnp.int32)
    positions = reverse_index(device_id * amp_dev + local_ids, local_bits + global_bits)
    totals = jax.tree.map(
        lambda part: one_axis_at_a_time(part, OUTER_INNER),
        check_terms(windowed, positions, angle_scale),
    )
    device_table = reversal_table(n_devices, global_bits)
    high_table = reversal_table(high_count, local_bits - global_bits)
    grid = windowed.reshape(2, high_count, n_devices)
    ordered = jnp.einsum("pm,shm->sph", device_table, grid, precision=lax.Precision.HIGHEST)
    blocks = ordered.reshape(2, n_outer, n_inner, high_count)
    blocks = exchange_both(blocks, OUTER_INNER, (OUTER, INNER), (1, 2), (1, 2))
    received = blocks.reshape(2, n_devices, high_count)
    turned_high = jnp.einsum("qh,sdh->sdq", high_table, received, precision=lax.Precision.HIGHEST)
    placed = jnp.einsum("ed,sdq->sqe", device_table, turned_high, precision=lax.Precision.HIGHEST)
    reversed_field = placed.reshape(2, amp_dev)
    mean_square = totals[0] / total_len
    factor = lax.rsqrt(mean_square + 1e-06)
    scaled = factor / math.sqrt(total_len)
    checks = jnp.stack([mean_square, totals[1] * scaled, totals[2] * scaled])
    return (reversed_field * factor, checks)


def solution(mesh):
    finer = Mesh(mesh.devices.reshape(4, 2, 4, 8), ("outer_0", "outer_1", "inner_0", "inner_1"))
    placed = (P(None, OUTER_INNER),)
    return jax.shard_map(
        per_device,
        mesh=finer,
        in_specs=placed,
        out_specs=(P(None, OUTER_INNER), P()),
        check_vma=False,
    )
```

profile of v0, /device:TPU:1, one launch (start us, length us, event | category | flops | bytes accessed | tf_op | source)
XLA Modules:
  0.0 125.0 jit_solution(6471467877127249729)
XLA Ops:
  0.7 0.0 copy-start.1
  0.7 5.3 %sine_multiply_fusion = (f32[512,512]{1,0:T(8,128)}, f32[512,512]{1,0:T(8,128)}, f32[512,512]{1,0:T(8,128)}) fusion(s32[512]{0:T(512)S(1)} %fusion.73), kind=kLoop, calls=%fused_computation.32 | loop fusion | flops 4456448 | bytes 3147776 | tf_op jit(solution)/shard_map/div | solution.py:83
  5.9 0.0 copy-done.1
  6.0 10.9 %slice_reduce_fusion.1 = (f32[262144]{0:T(1024)S(1)}, f32[262144]{0:T(1024)S(1)}) fusion(f32[2,262144]{1,0:T(2,128)S(1)} %copy-done.1), kind=kLoop, calls=%fused_computation.37 | loop fusion | bytes 4194304 | tf_op jit(solution)/shard_map/slice | solution.py:88
  16.9 0.2 reshape_squeeze.6
  17.1 0.2 reshape_squeeze.7
  17.2 10.1 %fusion = f32[512,1024]{1,0:T(8,128)S(1)} fusion(f32[512,512]{1,0:T(8,128)} %get-tuple-element.24, f32[512,512]{1,0:T(8,128)} %get-tuple-element.23, f32[512,512]{1,0:T(8,128)} %get-tuple-element.22, f32[512,512]{1,0:T(8,128)S(1)} %reshape_squeeze.7, f32[512,512]{1,0:T(8,128)S(1)} %reshape_squeeze.6), kind=kOutput, calls=%fused_computation | convolution fusion | flops 6446120960 | bytes 7340032 | tf_op jit(solution)/shard_map/dot_general | solution.py:90
  27.3 8.8 %add_reduce_fusion = (f32[]{:T(128)}, f32[]{:T(128)}, f32[1,1,512,512]{3,2,1,0:T(8,128)S(1)}, f32[1,1,512,512]{3,2,1,0:T(8,128)}, f32[512,512]{1,0:T(8,128)}, /*index=5*/f32[512,512]{1,0:T(8,128)S(1)}) fusion(s32[]{:T(128)S(6)} %mul.109, f32[512,1024]{1,0:T(8,128)S(1)} %fusion), kind=kLoop, calls=%fused_computation.30 | loop fusion | flops 30408704 | bytes 6291468 | tf_op jit(solution)/shard_map/reduce_sum | solution.py:60
  36.1 0.2 stack.21
  36.3 1.4 %stack.22 = f32[1,1024,256]{2,1,0:T(8,128)S(1)} reshape(f32[512,512]{1,0:T(8,128)} %get-tuple-element.20) | data formatting | bytes 2097152 | tf_op jit(solution)/shard_map/stack | solution.py:93
  37.7 1.3 %fusion.14 = f32[2,1024,256]{1,2,0:T(8,128)S(1)} fusion(f32[1,1024,256]{2,1,0:T(8,128)S(1)} %stack.22, f32[1,1024,256]{2,1,0:T(8,128)S(1)} %stack.21, s32[256]{0:T(256)S(1)} %fusion.106), kind=kOutput, calls=%fused_computation.14 | convolution fusion | flops 1611202560 | bytes 4195328 | tf_op jit(solution)/shard_map/pm,shm->sph/dot_general | solution.py:105
  39.0 2.9 %copy.3 = f32[8,32,2,1,1,1024]{5,2,1,0,4,3:T(2,128)} copy(f32[8,32,2,1,1,1024]{5,1,0,2,4,3:T(8,128)S(1)} %bitcast.41) | data formatting | bytes 4194304 | tf_op jit(solution)/shard_map/transpose;transpose | solution.py:35
  41.9 0.0 copy-start
  41.9 16.6 %all-to-all-start = ((f32[256,2,1,1,1024]{4,1,3,2,0:T(2,128)}), f32[256,2,1,1,1024]{4,1,3,2,0:T(2,128)}, u32[]{:S(2)}, u32[]{:S(2)}) async-start(f32[256,2,1,1,1024]{4,1,3,2,0:T(2,128)} %bitcast.6), calls=%async_computation | async-start | bytes 4194304 | tf_op jit(solution)/shard_map/all_to_all | solution.py:38
  58.6 0.0 copy-done
  58.6 1.1 copy.5
  59.7 1.1 copy.6
  60.8 2.8 %fusion.18 = f32[]{:T(128)} fusion(f32[1,262144]{1,0:T(1,128)S(1)} %bitcast.43, f32[1,262144]{1,0:T(1,128)S(1)} %bitcast.42), kind=kLoop, calls=%fused_computation.19 | loop fusion | flops 1572863 | bytes 2097156 | tf_op jit(solution)/shard_map/reduce_sum | solution.py:59
  63.5 10.4 %all-reduce.2 = (f32[]{:T(128)}, f32[]{:T(128)}, f32[]{:T(128)}) all-reduce(f32[]{:T(128)} %fusion.18, f32[]{:T(128)} %get-tuple-element.3, f32[]{:T(128)} %get-tuple-element.2), channel_id=1, replica_groups=mesh['outer_0'=4,'outer_1'=2,'inner_0'=4,'inner_1'=8] {'outer_0'}, use_global_device_ids=true, to_apply=%region_1.2 | all-reduce | flops 3 | bytes 24 | tf_op jit(solution)/shard_map/psum | solution.py:17
  73.9 4.0 %all-reduce.3 = (f32[]{:T(128)}, f32[]{:T(128)}, f32[]{:T(128)}) all-reduce(f32[]{:T(128)} %get-tuple-element.12, f32[]{:T(128)} %get-tuple-element.13, f32[]{:T(128)} %get-tuple-element.14), channel_id=1, replica_groups=mesh['outer_0'=4,'outer_1'=2,'inner_0'=4,'inner_1'=8] {'outer_1'}, use_global_device_ids=true, to_apply=%region_2.3 | all-reduce | flops 3 | bytes 24 | tf_op jit(solution)/shard_map/psum | solution.py:17
  78.0 9.9 %all-reduce.1 = (f32[]{:T(128)}, f32[]{:T(128)}, f32[]{:T(128)}) all-reduce(f32[]{:T(128)} %get-tuple-element.15, f32[]{:T(128)} %get-tuple-element.16, f32[]{:T(128)} %get-tuple-element.17), channel_id=1, replica_groups=mesh['outer_0'=4,'outer_1'=2,'inner_0'=4,'inner_1'=8] {'inner_0'}, use_global_device_ids=true, to_apply=%region_3.4 | all-reduce | flops 3 | bytes 24 | tf_op jit(solution)/shard_map/psum | solution.py:17
  87.9 25.1 %all-reduce = (f32[]{:T(128)}, f32[]{:T(128)}, f32[]{:T(128)}) all-reduce(f32[]{:T(128)} %get-tuple-element.9, f32[]{:T(128)} %get-tuple-element.10, f32[]{:T(128)} %get-tuple-element.11), channel_id=1, replica_groups=mesh['outer_0'=4,'outer_1'=2,'inner_0'=4,'inner_1'=8] {'inner_1'}, use_global_device_ids=true, to_apply=%region_4.5 | all-reduce | flops 3 | bytes 24 | tf_op jit(solution)/shard_map/psum | solution.py:17
  114.9 0.6 pad_maximum_fusion
  115.5 0.0 all-to-all-done
  115.5 5.4 %fusion.9 = f32[2,256,1024]{1,2,0:T(8,128)S(1)} fusion(f32[2,256,1024]{2,0,1:T(2,128)} %bitcast.11, s32[1024]{0:T(1024)S(1)} %fusion.45), kind=kOutput, calls=%fused_computation.10 | convolution fusion | flops 6443499520 | bytes 4198400 | tf_op jit(solution)/shard_map/qh,sdh->sdq/dot_general | solution.py:109
  120.9 1.2 multiply_bitcast_fusion
  122.1 2.9 %copy.7 = f32[1,2,1024,256]{3,1,2,0:T(2,128)} copy(f32[1,2,1024,256]{3,2,1,0:T(8,128)S(1)} %multiply_bitcast_fusion) | data formatting | bytes 4194304
  (3 shorter events, 0.0 us)
Async XLA Ops:
  0.7 5.3 %copy-start.1 = (f32[2,262144]{1,0:T(2,128)S(1)}, f32[2,262144]{1,0:T(2,128)}, u32[]{:S(2)}) copy-start(f32[2,262144]{1,0:T(2,128)} %param.1) | copy-start | bytes 6291460
  41.9 16.7 %copy-start = (f32[1,1,512,512]{3,2,1,0:T(8,128)S(1)}, f32[1,1,512,512]{3,2,1,0:T(8,128)}, u32[]{:S(2)}) copy-start(f32[1,1,512,512]{3,2,1,0:T(8,128)} %get-tuple-element.19) | copy-start | bytes 3145732
  41.9 73.6 %all-to-all-start = ((f32[256,2,1,1,1024]{4,1,3,2,0:T(2,128)}), f32[256,2,1,1,1024]{4,1,3,2,0:T(2,128)}, u32[]{:S(2)}, u32[]{:S(2)}) async-start(f32[256,2,1,1,1024]{4,1,3,2,0:T(2,128)} %bitcast.6), calls=%async_computation | async-start | bytes 4194304 | tf_op jit(solution)/shard_map/all_to_all | solution.py:38
where the time goes:
time: 127 us; the launch traced here: 125 us
  blocking collectives  49.4 us (39%)
  local copies, waits for them, and re-layouts  20.9 us (16%)
  matrix products  17.9 us (14%)
  other arithmetic  17.5 us (14%)
  starting transfers between devices  16.6 us (13%)
  between operations  2.7 us (2%)
    psum x4, blocking collectives, one_axis_at_a_time(): value = lax.psum(value, axis)  49.4 us
    all_to_all x1, starting transfers between devices, exchange_both(): parts = lax.all_to_all(parts, axis, split_axis=0, concat_axis=0, tiled=True)  16.6 us
    slice x1, local copies, waits for them, and re-layouts, per_device(): amplitudes[0].reshape(rows_count, columns)  10.9 us
    dot_general x1, matrix products, per_device(): jnp.dot(stacked, table, precision=lax.Precision.HIGHEST, preferred_elemen...  10.1 us
    reduce_sum x1, other arithmetic, check_terms(): phase_real = jnp.sum(current[0] * cosine + current[1] * sine)  8.83 us
    dot_general x1, matrix products, per_device(): jnp.einsum('qh,sdh->sdq', high_table, received, precision=lax.Precision.H...  5.37 us
    div x1, other arithmetic, per_device(): imag_part = jnp.sin(angles) / math.sqrt(columns)  5.26 us
    unnamed x7, local copies, waits for them, and re-layouts  5.11 us
  transfers between devices with their start and end apart: 1, of which 0 were waited for; matrix products, arithmetic and copies ran while one was open for 4% of the time, Pallas kernels for 0%

commit v1 on v0

v1 whole, which is shorter than its diff:
```python
import functools
import math

import jax
import jax.numpy as jnp
import numpy as np
from jax import lax
from jax.experimental import pallas as pl
from jax.experimental.pallas import tpu as pltpu
from jax.sharding import PartitionSpec as P

MESH = pl.DeviceIdType.MESH
AXES = ("outer", "inner")
AMP_DEV = 262144
DEVICES = 256
TOTAL = AMP_DEV * DEVICES
WINDOW = 512
ROWS = AMP_DEV // WINDOW
PITCH = 520


def dft_tables():
    e = np.arange(128)
    angle = 2.0 * np.pi * ((e[:, None] * e[None, :]) % 128) / 128.0
    cosine = np.cos(angle) / math.sqrt(WINDOW)
    sine = np.sin(angle) / math.sqrt(WINDOW)
    table = np.block([[cosine, -sine], [sine, cosine]]).astype(np.float32)
    high = table.astype(jnp.bfloat16)
    low = (table - high.astype(np.float32)).astype(jnp.bfloat16)
    twiddle = np.zeros((8, 128), np.float32)
    for g in (1, 2, 3):
        twiddle[2 * g - 2] = np.cos(2.0 * np.pi * g * e / WINDOW)
        twiddle[2 * g - 1] = np.sin(2.0 * np.pi * g * e / WINDOW)
    return high, low, twiddle


def reverse_bits(value, count):
    result = 0
    for bit in range(count):
        result = result + (value // 2**bit) % 2 * 2 ** (count - 1 - bit)
    return result


def exchange_kernel(
    x_ref, high_ref, low_ref, twiddle_ref, recv_ref, sums_ref,
    a_ref, bh_ref, bl_ref, send_ref, zsum_ref, xsum_ref, ysum_ref, csum_ref,
    load_sem, send_sem, recv_sem, round_sem, sum_send_sem, sum_recv_sem,
):
    outer, inner = lax.axis_index("outer"), lax.axis_index("inner")
    y, c, x, z = outer // 2, outer % 2, inner // 8, inner % 8
    me = outer * 32 + inner
    slot = reverse_bits(me, 8)

    def device(dy, dc, dx, dz):
        return ((y + dy) % 4 * 2 + (c + dc) % 2, (x + dx) % 4 * 8 + (z + dz) % 8)

    z_peers = [device(0, 0, 0, d) for d in range(1, 8)]
    x_peers = [device(0, 0, d, 0) for d in range(1, 4)]
    y_peers = [device(d, 0, 0, 0) for d in range(1, 4)]
    c_peers = [device(0, 1, 0, 0)]

    barrier = pltpu.get_barrier_semaphore()
    for peer in z_peers + x_peers + y_peers + c_peers:
        pl.semaphore_signal(barrier, inc=1, device_id=peer, device_id_type=MESH)

    loads = []
    for top in range(8):
        load = pltpu.make_async_copy(
            x_ref.at[pl.ds(512 * top, 512)],
            a_ref.at[pl.ds(PITCH * reverse_bits(top, 3), 512)],
            load_sem.at[top],
        )
        load.start()
        loads.append(load)
    for load in loads:
        load.wait()

    twiddles = [
        (twiddle_ref[pl.ds(2 * g - 2, 1), :], twiddle_ref[pl.ds(2 * g - 1, 1), :]) for g in (1, 2, 3)
    ]
    step = 2.0 * math.pi * 2048 / TOTAL
    cos_step, sin_step = math.cos(step), math.sin(step)

    def spread(turn, carry):
        squares, phase_real, phase_imag = carry
        h = 31 - turn
        row = reverse_bits(h, 5)
        parts = [
            [a_ref[pl.ds((row + 32 * b) * 8 + q, 8, stride=PITCH), :] for q in range(8)] for b in range(2)
        ]
        for b in (1, 0):
            phase_real, phase_imag = (
                phase_real * cos_step + phase_imag * sin_step + parts[b][0],
                phase_imag * cos_step - phase_real * sin_step + parts[b][1],
            )
            for q in range(8):
                squares = squares + parts[b][q] * parts[b][q]
        v = [jnp.concatenate([parts[0][q], parts[1][q]], 0) for q in range(8)]
        real, imag = v[0::2], v[1::2]
        s02r, s02i = real[0] + real[2], imag[0] + imag[2]
        d02r, d02i = real[0] - real[2], imag[0] - imag[2]
        s13r, s13i = real[1] + real[3], imag[1] + imag[3]
        d13r, d13i = real[1] - real[3], imag[1] - imag[3]
        u = [
            (s02r + s13r, s02i + s13i),
            (d02r - d13i, d02i + d13r),
            (s02r - s13r, s02i - s13i),
            (d02r + d13i, d02i - d13r),
        ]
        rows = pl.ds(pl.multiple_of(h * 16, 16), 16)
        for g in range(4):
            ur, ui = u[g]
            if g:
                cosine, sine = twiddles[g - 1]
                ur, ui = ur * cosine - ui * sine, ur * sine + ui * cosine
            for s, value in ((0, ur), (1, ui)):
                high = value.astype(jnp.bfloat16)
                low = (value - high.astype(jnp.float32)).astype(jnp.bfloat16)
                bh_ref[g, rows, 128 * s : 128 * s + 128] = high
                bl_ref[g, rows, 128 * s : 128 * s + 128] = low
        return squares, phase_real, phase_imag

    zero = jnp.zeros((8, 128), jnp.float32)
    squares, phase_real, phase_imag = lax.fori_loop(0, 32, spread, (zero, zero, zero))

    high, low = high_ref[...], low_ref[...]

    def transform(step, _):
        g, part = step // 2, step % 2
        rows = pl.ds(pl.multiple_of(part * 256, 256), 256)
        bh, bl = bh_ref[g, rows, :], bl_ref[g, rows, :]
        dims = (((1,), (1,)), ((), ()))
        out = (
            lax.dot_general(high, bh, dims, preferred_element_type=jnp.float32)
            + lax.dot_general(high, bl, dims, preferred_element_type=jnp.float32)
            + lax.dot_general(low, bh, dims, preferred_element_type=jnp.float32)
        )
        for s in range(2):
            for k in range(2):
                first = g // 2 * 1024 + (part * 2 + k) * 2 + s
                send_ref[g % 2, pl.ds(first, 128, stride=8), :] = out[
                    128 * s : 128 * s + 128, 128 * k : 128 * k + 128
                ]
        return 0

    lax.fori_loop(0, 8, transform, 0)

    lane = lax.broadcasted_iota(jnp.int32, (8, 128), 1)
    sub = lax.broadcasted_iota(jnp.int32, (8, 128), 0)
    angle = (sub * 256 + slot).astype(jnp.float32) * (2.0 * math.pi / TOTAL)
    cosine, sine = jnp.cos(angle), jnp.sin(angle)
    turned_real = jnp.where(lane == 1, phase_real * cosine + phase_imag * sine, 0.0)
    turned_imag = jnp.where(lane == 1, phase_imag * cosine - phase_real * sine, 0.0)
    mine = jnp.where(
        sub == 0,
        jnp.sum(squares, 0, keepdims=True),
        jnp.where(
            sub == 1,
            jnp.sum(turned_real, 0, keepdims=True),
            jnp.where(sub == 2, jnp.sum(turned_imag, 0, keepdims=True), 0.0),
        ),
    )

    pl.semaphore_wait(barrier, 14)
    for number, peers in enumerate((x_peers, y_peers, c_peers)):
        for peer in peers:
            pl.semaphore_signal(round_sem.at[number], inc=1, device_id=peer, device_id_type=MESH)
        pl.semaphore_wait(round_sem.at[number], len(peers))

    def copy(peer, source, target, number):
        return pltpu.make_async_remote_copy(
            src_ref=source,
            dst_ref=target,
            send_sem=sum_send_sem.at[number],
            recv_sem=sum_recv_sem.at[number],
            device_id=peer,
            device_id_type=MESH,
        )

    def bulk(peer, at):
        return pltpu.make_async_remote_copy(
            src_ref=send_ref.at[:, pl.ds(pl.multiple_of(at * 8, 8), 8)],
            dst_ref=recv_ref.at[:, pl.ds(pl.multiple_of(slot * 8, 8), 8)],
            send_sem=send_sem,
            recv_sem=recv_sem,
            device_id=peer,
            device_id_type=MESH,
        )

    def send_bulk(first, last):
        def body(t, _):
            dz, dx, dc, dy = t % 8, t // 8 % 4, t // 32 % 2, t // 64
            peer = device(dy, dc, dx, dz)
            target = peer[0] * 32 + peer[1]
            bulk(peer, target % 2 * 128 + target // 2).start()
            return 0

        lax.fori_loop(first, last, body, 0)

    total = mine
    for number, (peers, place, buffer, first) in enumerate((
        (z_peers, z, zsum_ref, 1),
        (x_peers, x, xsum_ref, 64),
        (y_peers, y, ysum_ref, 128),
        (c_peers, c, csum_ref, 192),
    )):
        buffer[place] = total
        for peer in peers:
            copy(peer, buffer.at[place], buffer.at[place], number).start()
        send_bulk(first, 64 * number + 64)
        if number == 0:
            own = pl.multiple_of((me % 2 * 128 + me // 2) * 8, 8)
            recv_ref[:, pl.ds(pl.multiple_of(slot * 8, 8), 8), :] = send_ref[:, pl.ds(own, 8), :]
        n = len(peers)
        done = copy(peers[0], buffer.at[pl.ds(0, n)], buffer.at[pl.ds(0, n)], number)
        done.wait_recv()
        done.wait_send()
        total = buffer[0]
        for i in range(1, n + 1):
            total = total + buffer[i]
    sums_ref[...] = total

    done = pltpu.make_async_remote_copy(
        src_ref=send_ref.at[:, pl.ds(0, 2040)],
        dst_ref=recv_ref.at[:, pl.ds(0, 2040)],
        send_sem=send_sem,
        recv_sem=recv_sem,
        device_id=c_peers[0],
        device_id_type=MESH,
    )
    done.wait_recv()
    done.wait_send()


def place_kernel(recv_ref, sums_ref, out_ref, checks_ref):
    step = pl.program_id(0)
    half, part = step // 4, step % 4
    mean_square = jnp.sum(sums_ref[pl.ds(0, 1), :], axis=1, keepdims=True) / TOTAL
    factor = lax.rsqrt(mean_square + 1e-06)
    for s in range(2):
        for d in range(2):
            block = recv_ref[half, pl.ds(d * 1024 + part * 2 + s, 128, stride=8), :]
            out_ref[pl.ds(d * 2 + s, 128, stride=4), :] = block.T * factor

    @pl.when(step == 0)
    def _():
        scale = factor * (math.sqrt(WINDOW) / math.sqrt(TOTAL))
        checks_ref[0] = mean_square[0, 0]
        for i in (1, 2):
            value = jnp.sum(sums_ref[pl.ds(i, 1), :], axis=1, keepdims=True) * scale
            checks_ref[i] = value[0, 0]


def per_device(amplitudes):
    high, low, twiddle = dft_tables()
    rows = amplitudes.reshape(2, 2048, 128).transpose(1, 0, 2).reshape(4096, 128)
    vmem = pl.BlockSpec(memory_space=pltpu.VMEM)
    recv, sums = pl.pallas_call(
        exchange_kernel,
        out_shape=(
            jax.ShapeDtypeStruct((2, 2048, 128), jnp.float32),
            jax.ShapeDtypeStruct((8, 128), jnp.float32),
        ),
        in_specs=[pl.BlockSpec(memory_space=pl.ANY), vmem, vmem, vmem],
        out_specs=(vmem, vmem),
        scratch_shapes=[
            pltpu.VMEM((8 * PITCH, 128), jnp.float32),
            pltpu.VMEM((4, 512, 256), jnp.bfloat16),
            pltpu.VMEM((4, 512, 256), jnp.bfloat16),
            pltpu.VMEM((2, 2048, 128), jnp.float32),
            pltpu.VMEM((8, 8, 128), jnp.float32),
            pltpu.VMEM((4, 8, 128), jnp.float32),
            pltpu.VMEM((4, 8, 128), jnp.float32),
            pltpu.VMEM((2, 8, 128), jnp.float32),
            pltpu.SemaphoreType.DMA((8,)),
            pltpu.SemaphoreType.DMA,
            pltpu.SemaphoreType.DMA,
            pltpu.SemaphoreType.REGULAR((3,)),
            pltpu.SemaphoreType.DMA((4,)),
            pltpu.SemaphoreType.DMA((4,)),
        ],
        compiler_params=pltpu.CompilerParams(
            collective_id=1, has_side_effects=True, vmem_limit_bytes=24 * 1024 * 1024
        ),
    )(rows, jnp.asarray(high), jnp.asarray(low), jnp.asarray(twiddle))
    placed, checks = pl.pallas_call(
        place_kernel,
        grid=(8,),
        out_shape=(
            jax.ShapeDtypeStruct((4096, 128), jnp.float32),
            jax.ShapeDtypeStruct((3,), jnp.float32),
        ),
        in_specs=[vmem, vmem],
        out_specs=(
            pl.BlockSpec((512, 128), lambda i: (i, 0)),
            pl.BlockSpec(memory_space=pltpu.SMEM),
        ),
        compiler_params=pltpu.CompilerParams(vmem_limit_bytes=16 * 1024 * 1024),
    )(recv, sums)
    transformed = placed.reshape(2048, 2, 128).transpose(1, 0, 2).reshape(2, AMP_DEV)
    return transformed, checks


def solution(mesh):
    return jax.shard_map(
        per_device,
        mesh=mesh,
        in_specs=(P(None, AXES),),
        out_specs=(P(None, AXES), P()),
        check_vma=False,
    )
```

time: 127 us -> 74.8 us (0.59); the launches traced: 125 us -> 74.6 us
  Pallas kernels: 0 us -> 69.9 us
  blocking collectives: 49.4 us -> 0 us
  matrix products: 17.9 us -> 0 us
  other arithmetic: 17.5 us -> 0 us
  local copies, waits for them, and re-layouts: 20.9 us -> 4.08 us
  starting transfers between devices: 16.6 us -> 0 us
  between operations: 2.7 us -> 0.65 us
    pallas_call x0 -> x2, Pallas kernels: none -> 69.9 us  [the longest x1 66.1 us: per_device(): pl.pallas_call(exchange_kernel, out_shape=(jax.ShapeDtypeStruct((2, 2048,...]
    psum x4 -> x0, blocking collectives: 49.4 us -> none  [one_axis_at_a_time(): value = lax.psum(value, axis)]
    dot_general x4 -> x0, matrix products: 17.9 us -> none  [the longest x1 10.1 us: per_device(): jnp.dot(stacked, table, precision=lax.Precision.HIGHEST, preferred_elemen...]
    all_to_all x1 -> x0, starting transfers between devices: 16.6 us -> none  [exchange_both(): parts = lax.all_to_all(parts, axis, split_axis=0, concat_axis=0, tiled=True)]
    reduce_sum x2 -> x0, other arithmetic: 11.6 us -> none  [the longest x1 8.83 us: check_terms(): phase_real = jnp.sum(current[0] * cosine + current[1] * sine)]
    slice x1 -> x0, local copies, waits for them, and re-layouts: 10.9 us -> none  [per_device(): amplitudes[0].reshape(rows_count, columns)]
    div x1 -> x0, other arithmetic: 5.26 us -> none  [per_device(): imag_part = jnp.sin(angles) / math.sqrt(columns)]
    another operation x5 -> x0, local copies, waits for them, and re-layouts: 4.82 us -> none  [the longest x1 2.94 us: exchange_both(): parts = jnp.moveaxis(cut_along(parts, splits[1] + 1, sizes[1]), 0, 1)]
  transfers between devices with their start and end apart: 1 -> 0, of which waited for: 0 -> 0; matrix products, arithmetic and copies ran while one was open for 4% -> 0% of each run, Pallas kernels for 0% -> 0%
where the time goes in v1:
time: 74.8 us; the launch traced here: 74.6 us
  Pallas kernels  69.9 us (93%)
  local copies, waits for them, and re-layouts  4.08 us (5%)
    pallas_call x1, Pallas kernels, per_device(): pl.pallas_call(exchange_kernel, out_shape=(jax.ShapeDtypeStruct((2, 2048,...  66.1 us
    unnamed x8, local copies, waits for them, and re-layouts  4.08 us
    pallas_call x1, Pallas kernels, per_device(): pl.pallas_call(place_kernel, grid=(8,), out_shape=(jax.ShapeDtypeStruct((...  3.77 us

profile of v1, /device:TPU:1, one launch (start us, length us, event | category | flops | bytes accessed | tf_op | source)
XLA Modules:
  0.0 74.6 jit_solution(15135383296095650102)
XLA Ops:
  0.6 0.0 copy-start
  0.6 1.6 %copy-done = f32[2,262144]{1,0:T(2,128)S(1)} copy-done((f32[2,262144]{1,0:T(2,128)S(1)}, f32[2,262144]{1,0:T(2,128)}, u32[]{:S(2)}) %copy-start) | copy-done | bytes 2097176
  2.2 0.0 copy-start.1
  2.2 0.9 %copy-done.1 = bf16[256,256]{1,0:T(8,128)(2,1)S(1)} copy-done((bf16[256,256]{1,0:T(8,128)(2,1)S(1)}, bf16[256,256]{1,0:T(8,128)(2,1)}, u32[]{:S(2)}) %copy-start.1) | copy-done | bytes 131096
  3.1 0.0 copy-start.2
  3.1 0.9 %copy-done.2 = bf16[256,256]{1,0:T(8,128)(2,1)S(1)} copy-done((bf16[256,256]{1,0:T(8,128)(2,1)S(1)}, bf16[256,256]{1,0:T(8,128)(2,1)}, u32[]{:S(2)}) %copy-start.2) | copy-done | bytes 131096
  4.0 0.0 copy-start.3
  4.0 0.7 copy-done.3
  4.7 66.1 %shard_map.59 = (f32[2,2048,128]{2,1,0:T(8,128)S(1)}, f32[8,128]{1,0:T(8,128)S(1)}) custom-call(f32[4096,128]{1,0:T(8,128)S(1)} %bitcast.10, bf16[256,256]{1,0:T(8,128)(2,1)S(1)} %copy-done.2, bf16[256,256]{1,0:T(8,128)(2,1)S(1)} %copy-done.1, f32[8,128]{1,0:T(8,128)S(1)} %copy-done.3), custom_call_target="tpu_custom_call" | custom-call | tf_op jit(solution)/shard_map/pallas_call | solution.py:258
  70.8 3.8 %shard_map.60 = (f32[4096,128]{1,0:T(8,128)}, f32[3]{0:T(128)}) custom-call(f32[2,2048,128]{2,1,0:T(8,128)S(1)} %get-tuple-element.6.recv_ref, f32[8,128]{1,0:T(8,128)S(1)} %get-tuple-element.7.sums_ref), custom_call_target="tpu_custom_call" | custom-call | tf_op jit(solution)/shard_map/pallas_call | solution.py:286
Async XLA Ops:
  0.6 1.6 %copy-start = (f32[2,262144]{1,0:T(2,128)S(1)}, f32[2,262144]{1,0:T(2,128)}, u32[]{:S(2)}) copy-start(f32[2,262144]{1,0:T(2,128)} %param.4) | copy-start | bytes 6291460
  2.2 0.9 %copy-start.1 = (bf16[256,256]{1,0:T(8,128)(2,1)S(1)}, bf16[256,256]{1,0:T(8,128)(2,1)}, u32[]{:S(2)}) copy-start(bf16[256,256]{1,0:T(8,128)(2,1)} %constant.7.clone.low_ref) | copy-start | bytes 393220
  3.1 0.9 %copy-start.2 = (bf16[256,256]{1,0:T(8,128)(2,1)S(1)}, bf16[256,256]{1,0:T(8,128)(2,1)}, u32[]{:S(2)}) copy-start(bf16[256,256]{1,0:T(8,128)(2,1)} %constant.6.clone.high_ref) | copy-start | bytes 393220
  4.0 0.7 copy-start.3

commit v2 on v1

v2 whole, which is shorter than its diff:
```python
import math

import jax
import jax.numpy as jnp
import numpy as np
from jax import lax
from jax.experimental import pallas as pl
from jax.experimental.pallas import tpu as pltpu
from jax.sharding import PartitionSpec as P

MESH = pl.DeviceIdType.MESH
AXES = ("outer", "inner")
AMP_DEV = 262144
DEVICES = 256
TOTAL = AMP_DEV * DEVICES
WINDOW = 512
PITCH = 520


def dft_tables():
    e = np.arange(128)
    frequency = e % 32 * 4 + e // 32
    angle = 2.0 * np.pi * ((frequency[:, None] * e[None, :]) % 128) / 128.0
    cosine = np.cos(angle) / math.sqrt(WINDOW)
    sine = np.sin(angle) / math.sqrt(WINDOW)
    table = np.block([[cosine, -sine], [sine, cosine]]).astype(np.float32)
    high = table.astype(jnp.bfloat16)
    low = (table - high.astype(np.float32)).astype(jnp.bfloat16)
    twiddle = np.zeros((8, 128), np.float32)
    for g in (1, 2, 3):
        twiddle[2 * g - 2] = np.cos(2.0 * np.pi * g * e / WINDOW)
        twiddle[2 * g - 1] = np.sin(2.0 * np.pi * g * e / WINDOW)
    return high, low, twiddle


def reverse_bits(value, count):
    result = 0
    for bit in range(count):
        result = result + (value // 2**bit) % 2 * 2 ** (count - 1 - bit)
    return result


def scale_factor(sums_row):
    mean_square = jnp.sum(sums_row, axis=1, keepdims=True) / TOTAL
    return mean_square, lax.rsqrt(mean_square + 1e-06)


def exchange_kernel(
    x_hbm, high_hbm, low_hbm, twiddle_hbm, placed_ref, odd_ref, sums_ref,
    a_ref, high_ref, low_ref, twiddle_ref, bh_ref, bl_ref,
    send_ref, mid_a_ref, mid_b_ref, even_ref, zsum_ref, psum_ref,
    load_sem, table_sem, send_sem, recv_sem,
):
    outer, inner = lax.axis_index("outer"), lax.axis_index("inner")
    y, c, x, z = outer // 2, outer % 2, inner // 8, inner % 8
    plane = outer * 4 + x
    z_slot, p_slot = reverse_bits(z, 3), reverse_bits(plane, 5)
    z_index = z % 2 * 4 + z // 2
    slot = z_slot * 32 + p_slot

    def z_peer(there):
        return (outer, x * 8 + there)

    def plane_peer(t):
        dx, dc, dy = t % 4, t // 4 % 2, t // 8
        there_outer, there_x = (y + dy) % 4 * 2 + (c + dc) % 2, (x + dx) % 4
        return (there_outer, there_x * 8 + z), there_outer * 4 + there_x

    loads = []
    for number, (source, target) in enumerate((
        (high_hbm, high_ref), (low_hbm, low_ref), (twiddle_hbm, twiddle_ref),
    )):
        loads.append(pltpu.make_async_copy(source, target, table_sem.at[number]))
    for top in range(8):
        loads.append(
            pltpu.make_async_copy(
                x_hbm.at[pl.ds(512 * top, 512)],
                a_ref.at[pl.ds(PITCH * reverse_bits(top, 3), 512)],
                load_sem.at[top],
            )
        )
    for load in loads:
        load.start()

    barrier = pltpu.get_barrier_semaphore()
    for d in range(1, 8):
        pl.semaphore_signal(barrier, inc=1, device_id=z_peer((z + d) % 8), device_id_type=MESH)

    def greet(t, _):
        pl.semaphore_signal(barrier, inc=1, device_id=plane_peer(t)[0], device_id_type=MESH)
        return 0

    lax.fori_loop(1, 32, greet, 0)

    for load in loads:
        load.wait()

    twiddles = [
        (twiddle_ref[pl.ds(2 * g - 2, 1), :], twiddle_ref[pl.ds(2 * g - 1, 1), :]) for g in (1, 2, 3)
    ]
    step = 2.0 * math.pi * 2048 / TOTAL
    cos_step, sin_step = math.cos(step), math.sin(step)

    def spread(turn, carry):
        squares, phase_real, phase_imag = carry
        h = 31 - turn
        row = reverse_bits(h, 5)
        parts = [
            [a_ref[pl.ds((row + 32 * b) * 8 + q, 8, stride=PITCH), :] for q in range(8)] for b in range(2)
        ]
        for b in (1, 0):
            phase_real, phase_imag = (
                phase_real * cos_step + phase_imag * sin_step + parts[b][0],
                phase_imag * cos_step - phase_real * sin_step + parts[b][1],
            )
            for q in range(8):
                squares = squares + parts[b][q] * parts[b][q]
        v = [jnp.concatenate([parts[0][q], parts[1][q]], 0) for q in range(8)]
        real, imag = v[0::2], v[1::2]
        s02r, s02i = real[0] + real[2], imag[0] + imag[2]
        d02r, d02i = real[0] - real[2], imag[0] - imag[2]
        s13r, s13i = real[1] + real[3], imag[1] + imag[3]
        d13r, d13i = real[1] - real[3], imag[1] - imag[3]
        u = [
            (s02r + s13r, s02i + s13i),
            (d02r - d13i, d02i + d13r),
            (s02r - s13r, s02i - s13i),
            (d02r + d13i, d02i - d13r),
        ]
        rows = pl.ds(pl.multiple_of(h * 16, 16), 16)
        for g in range(4):
            ur, ui = u[g]
            if g:
                cosine, sine = twiddles[g - 1]
                ur, ui = ur * cosine - ui * sine, ur * sine + ui * cosine
            for s, value in ((0, ur), (1, ui)):
                high = value.astype(jnp.bfloat16)
                low = (value - high.astype(jnp.float32)).astype(jnp.bfloat16)
                bh_ref[g, rows, 128 * s : 128 * s + 128] = high
                bl_ref[g, rows, 128 * s : 128 * s + 128] = low
        return squares, phase_real, phase_imag

    zero = jnp.zeros((8, 128), jnp.float32)
    squares, phase_real, phase_imag = lax.fori_loop(0, 32, spread, (zero, zero, zero))

    lane = lax.broadcasted_iota(jnp.int32, (8, 128), 1)
    sub = lax.broadcasted_iota(jnp.int32, (8, 128), 0)
    angle = (sub * 256 + slot).astype(jnp.float32) * (2.0 * math.pi / TOTAL)
    cosine, sine = jnp.cos(angle), jnp.sin(angle)
    turned_real = jnp.where(lane == 1, phase_real * cosine + phase_imag * sine, 0.0)
    turned_imag = jnp.where(lane == 1, phase_imag * cosine - phase_real * sine, 0.0)
    mine = jnp.where(
        sub == 0,
        jnp.sum(squares, 0, keepdims=True),
        jnp.where(
            sub == 1,
            jnp.sum(turned_real, 0, keepdims=True),
            jnp.where(sub == 2, jnp.sum(turned_imag, 0, keepdims=True), 0.0),
        ),
    )
    zsum_ref[z] = mine

    def transform(g):
        def body(part, _):
            rows = pl.ds(pl.multiple_of(part * 256, 256), 256)
            bh, bl = bh_ref[g, rows, :], bl_ref[g, rows, :]
            dims = (((1,), (1,)), ((), ()))
            out = (
                lax.dot_general(high_ref[...], bh, dims, preferred_element_type=jnp.float32)
                + lax.dot_general(high_ref[...], bl, dims, preferred_element_type=jnp.float32)
                + lax.dot_general(low_ref[...], bh, dims, preferred_element_type=jnp.float32)
            )
            for s in range(2):
                for k in range(2):
                    first = g // 2 * 1024 + (part * 2 + k) * 2 + s
                    send_ref[g % 2, pl.ds(first, 128, stride=8), :] = out[
                        128 * s : 128 * s + 128, 128 * k : 128 * k + 128
                    ]
            return 0

        lax.fori_loop(0, 2, body, 0)

    def copy(peer, source, target, number):
        return pltpu.make_async_remote_copy(
            src_ref=source,
            dst_ref=target,
            send_sem=send_sem.at[number],
            recv_sem=recv_sem.at[number],
            device_id=peer,
            device_id_type=MESH,
        )

    def finish_recv(ref, number):
        copy(z_peer((z + 1) % 8), ref, ref, number).wait_recv()

    def finish_send(ref, number):
        copy(z_peer((z + 1) % 8), ref, ref, number).wait_send()

    even_send = send_ref.reshape(2, 8, 32, 8, 128).at[0]
    odd_send = send_ref.reshape(2, 8, 32, 8, 128).at[1]

    transform(0)
    pl.semaphore_wait(barrier, 38)
    for d in range(1, 8):
        copy(z_peer((z + d) % 8), zsum_ref.at[z], zsum_ref.at[z], 0).start()
    for parity in range(2):
        if parity:
            transform(2)
        for high_part in range(4):
            there = 2 * high_part + parity

            @pl.when(there != z)
            def _():
                copy(z_peer(there), even_send.at[4 * parity + high_part], mid_a_ref.at[z_slot], 1).start()

    transform(1)
    transform(3)

    def plane_bulk(source, target, number):
        def body(t, _):
            peer, there = plane_peer(t)
            copy(peer, source.at[:, there], target.at[:, p_slot], number).start()
            return 0

        lax.fori_loop(1, 32, body, 0)

    plane_bulk(odd_send, mid_b_ref, 2)
    mid_a_ref[z_slot] = even_send[z_index]
    for i in range(8):
        mid_b_ref[i, p_slot] = odd_send[i, plane]

    finish_recv(zsum_ref.at[pl.ds(0, 7)], 0)
    total = zsum_ref[0]
    for i in range(1, 8):
        total = total + zsum_ref[i]
    psum_ref[plane] = total

    def plane_sums(t, _):
        copy(plane_peer(t)[0], psum_ref.at[plane], psum_ref.at[plane], 3).start()
        return 0

    lax.fori_loop(1, 32, plane_sums, 0)

    finish_recv(mid_b_ref.at[:, pl.ds(0, 31)], 2)
    for d in (4, 3, 5, 2, 6, 1, 7):
        there = (z + d) % 8
        copy(z_peer(there), mid_b_ref.at[there % 2 * 4 + there // 2], odd_ref.at[z_slot], 4).start()
    odd_ref[z_slot] = mid_b_ref[z_index]

    finish_recv(psum_ref.at[pl.ds(0, 31)], 3)
    total = psum_ref[0]
    for i in range(1, 32):
        total = total + psum_ref[i]
    sums_ref[...] = total
    factor = scale_factor(total[0:1])[1]

    finish_recv(mid_a_ref.at[pl.ds(0, 7)], 1)
    plane_bulk(mid_a_ref, even_ref, 5)
    for i in range(8):
        even_ref[i, p_slot] = mid_a_ref[i, plane]
    finish_recv(even_ref.at[:, pl.ds(0, 31)], 5)
    even_rows = even_ref.reshape(2048, 128)

    def place(part, _):
        for s in range(2):
            for d in range(2):
                block = even_rows[pl.ds(d * 1024 + part * 2 + s, 128, stride=8), :]
                placed_ref[pl.ds(part * 512 + d * 2 + s, 128, stride=4), :] = block.T * factor
        return 0

    lax.fori_loop(0, 4, place, 0)

    finish_recv(odd_ref.at[pl.ds(0, 7)], 4)
    finish_send(zsum_ref.at[pl.ds(0, 7)], 0)
    finish_send(mid_a_ref.at[pl.ds(0, 7)], 1)
    finish_send(mid_b_ref.at[:, pl.ds(0, 31)], 2)
    finish_send(psum_ref.at[pl.ds(0, 31)], 3)
    finish_send(mid_b_ref.at[pl.ds(0, 7)], 4)
    finish_send(even_ref.at[:, pl.ds(0, 31)], 5)


def place_kernel(placed_ref, odd_ref, sums_ref, out_hbm, checks_ref, buffer_ref, sems):
    copies = [pltpu.make_async_copy(placed_ref, out_hbm.at[pl.ds(0, 2048)], sems.at[4])]
    copies[0].start()
    mean_square, factor = scale_factor(sums_ref[pl.ds(0, 1), :])
    for part in range(4):
        for s in range(2):
            for d in range(2):
                block = odd_ref[pl.ds(d * 1024 + part * 2 + s, 128, stride=8), :]
                buffer_ref[pl.ds(part * 512 + d * 2 + s, 128, stride=4), :] = block.T * factor
        copies.append(
            pltpu.make_async_copy(
                buffer_ref.at[pl.ds(part * 512, 512)],
                out_hbm.at[pl.ds(2048 + part * 512, 512)],
                sems.at[part],
            )
        )
        copies[-1].start()
    scale = factor * (math.sqrt(WINDOW) / math.sqrt(TOTAL))
    checks_ref[0] = mean_square[0, 0]
    for i in (1, 2):
        value = jnp.sum(sums_ref[pl.ds(i, 1), :], axis=1, keepdims=True) * scale
        checks_ref[i] = value[0, 0]
    for moved in copies:
        moved.wait()


def per_device(amplitudes):
    high, low, twiddle = dft_tables()
    rows = amplitudes.reshape(2, 2048, 128).transpose(1, 0, 2).reshape(4096, 128)
    vmem = pl.BlockSpec(memory_space=pltpu.VMEM)
    hbm = pl.BlockSpec(memory_space=pltpu.HBM)
    f32, bf16 = jnp.float32, jnp.bfloat16
    placed, odd, sums = pl.pallas_call(
        exchange_kernel,
        out_shape=(
            jax.ShapeDtypeStruct((2048, 128), f32),
            jax.ShapeDtypeStruct((8, 32, 8, 128), f32),
            jax.ShapeDtypeStruct((8, 128), f32),
        ),
        in_specs=[hbm, hbm, hbm, hbm],
        out_specs=(vmem, vmem, vmem),
        scratch_shapes=[
            pltpu.VMEM((8 * PITCH, 128), f32),
            pltpu.VMEM((256, 256), bf16),
            pltpu.VMEM((256, 256), bf16),
            pltpu.VMEM((8, 128), f32),
            pltpu.VMEM((4, 512, 256), bf16),
            pltpu.VMEM((4, 512, 256), bf16),
            pltpu.VMEM((2, 2048, 128), f32),
            pltpu.VMEM((8, 32, 8, 128), f32),
            pltpu.VMEM((8, 32, 8, 128), f32),
            pltpu.VMEM((8, 32, 8, 128), f32),
            pltpu.VMEM((8, 8, 128), f32),
            pltpu.VMEM((32, 8, 128), f32),
            pltpu.SemaphoreType.DMA((8,)),
            pltpu.SemaphoreType.DMA((3,)),
            pltpu.SemaphoreType.DMA((6,)),
            pltpu.SemaphoreType.DMA((6,)),
        ],
        compiler_params=pltpu.CompilerParams(
            collective_id=1, has_side_effects=True, vmem_limit_bytes=24 * 1024 * 1024
        ),
    )(rows, jnp.asarray(high), jnp.asarray(low), jnp.asarray(twiddle))
    out, checks = pl.pallas_call(
        place_kernel,
        out_shape=(
            jax.ShapeDtypeStruct((4096, 128), f32),
            jax.ShapeDtypeStruct((3,), f32),
        ),
        in_specs=[vmem, vmem, vmem],
        out_specs=(hbm, pl.BlockSpec(memory_space=pltpu.SMEM)),
        scratch_shapes=[pltpu.VMEM((2048, 128), f32), pltpu.SemaphoreType.DMA((5,))],
        compiler_params=pltpu.CompilerParams(vmem_limit_bytes=16 * 1024 * 1024),
    )(placed, odd.reshape(2048, 128), sums)
    transformed = out.reshape(2048, 2, 128).transpose(1, 0, 2).reshape(2, AMP_DEV)
    return transformed, checks


def solution(mesh):
    return jax.shard_map(
        per_device,
        mesh=mesh,
        in_specs=(P(None, AXES),),
        out_specs=(P(None, AXES), P()),
        check_vma=False,
    )
```

time: 74.8 us -> 67 us (0.90)
  Pallas kernels: 69.9 us -> 62.1 us
    pallas_call x2, Pallas kernels: 69.9 us -> 62.1 us  [the longest x1 60.2 us: per_device(): pl.pallas_call(exchange_kernel, out_shape=(jax.ShapeDtypeStruct((2048, 12...]
where the time goes in v2:
time: 67 us; the launch traced here: 66.8 us
  Pallas kernels  62.1 us (93%)
  local copies, waits for them, and re-layouts  4.08 us (6%)
    pallas_call x1, Pallas kernels, per_device(): pl.pallas_call(exchange_kernel, out_shape=(jax.ShapeDtypeStruct((2048, 12...  60.2 us
    unnamed x8, local copies, waits for them, and re-layouts  4.08 us
    pallas_call x1, Pallas kernels, per_device(): pl.pallas_call(place_kernel, out_shape=(jax.ShapeDtypeStruct((4096, 128),...  1.87 us

profile of v2, /device:TPU:1, one launch (start us, length us, event | category | flops | bytes accessed | tf_op | source)
XLA Modules:
  0.0 66.8 jit_solution(18182931703170400959)
XLA Ops:
  0.6 0.0 copy-start
  0.6 1.6 %copy-done = f32[2,262144]{1,0:T(2,128)S(1)} copy-done((f32[2,262144]{1,0:T(2,128)S(1)}, f32[2,262144]{1,0:T(2,128)}, u32[]{:S(2)}) %copy-start) | copy-done | bytes 2097176
  2.2 0.0 copy-start.1
  2.2 0.9 %copy-done.1 = bf16[256,256]{1,0:T(8,128)(2,1)S(1)} copy-done((bf16[256,256]{1,0:T(8,128)(2,1)S(1)}, bf16[256,256]{1,0:T(8,128)(2,1)}, u32[]{:S(2)}) %copy-start.1) | copy-done | bytes 131096
  3.1 0.0 copy-start.2
  3.1 0.9 %copy-done.2 = bf16[256,256]{1,0:T(8,128)(2,1)S(1)} copy-done((bf16[256,256]{1,0:T(8,128)(2,1)S(1)}, bf16[256,256]{1,0:T(8,128)(2,1)}, u32[]{:S(2)}) %copy-start.2) | copy-done | bytes 131096
  4.0 0.0 copy-start.3
  4.0 0.7 %copy-done.3 = f32[8,128]{1,0:T(8,128)S(1)} copy-done((f32[8,128]{1,0:T(8,128)S(1)}, f32[8,128]{1,0:T(8,128)}, u32[]{:S(2)}) %copy-start.3) | copy-done | bytes 4120
  4.7 60.2 %shard_map.59 = (f32[2048,128]{1,0:T(8,128)S(1)}, f32[8,32,8,128]{3,2,1,0:T(8,128)S(1)}, f32[8,128]{1,0:T(8,128)S(1)}) custom-call(f32[4096,128]{1,0:T(8,128)S(1)} %bitcast.11, bf16[256,256]{1,0:T(8,128)(2,1)S(1)} %copy-done.2, bf16[256,256]{1,0:T(8,128)(2,1)S(1)} %copy-done.1, f32[8,128]{1,0:T(8,128)S(1)} %copy-done.3), custom_call_target="tpu_custom_call" | custom-call | tf_op jit(solution)/shard_map/pallas_call | solution.py:314
  65.0 1.9 %shard_map.60 = (f32[4096,128]{1,0:T(8,128)}, f32[3]{0:T(128)}) custom-call(f32[2048,128]{1,0:T(8,128)S(1)} %get-tuple-element.7.placed_ref, f32[2048,128]{1,0:T(8,128)S(1)} %bitcast.12, f32[8,128]{1,0:T(8,128)S(1)} %get-tuple-element.9.sums_ref), custom_call_target="tpu_custom_call" | custom-call | tf_op jit(solution)/shard_map/pallas_call | solution.py:345
Async XLA Ops:
  0.6 1.6 %copy-start = (f32[2,262144]{1,0:T(2,128)S(1)}, f32[2,262144]{1,0:T(2,128)}, u32[]{:S(2)}) copy-start(f32[2,262144]{1,0:T(2,128)} %param.4) | copy-start | bytes 6291460
  2.2 0.9 %copy-start.1 = (bf16[256,256]{1,0:T(8,128)(2,1)S(1)}, bf16[256,256]{1,0:T(8,128)(2,1)}, u32[]{:S(2)}) copy-start(bf16[256,256]{1,0:T(8,128)(2,1)} %constant.7.clone.low_hbm) | copy-start | bytes 393220
  3.1 0.9 %copy-start.2 = (bf16[256,256]{1,0:T(8,128)(2,1)S(1)}, bf16[256,256]{1,0:T(8,128)(2,1)}, u32[]{:S(2)}) copy-start(bf16[256,256]{1,0:T(8,128)(2,1)} %constant.6.clone.high_hbm) | copy-start | bytes 393220
  4.0 0.7 %copy-start.3 = (f32[8,128]{1,0:T(8,128)S(1)}, f32[8,128]{1,0:T(8,128)}, u32[]{:S(2)}) copy-start(f32[8,128]{1,0:T(8,128)} %constant.8.clone.twiddle_hbm) | copy-start | bytes 12292

commit v3 on v2

v3 whole, which is shorter than its diff:
```python
import math

import jax
import jax.numpy as jnp
from jax import lax
from jax.experimental import pallas as pl
from jax.experimental.pallas import tpu as pltpu
from jax.sharding import PartitionSpec as P

MESH = pl.DeviceIdType.MESH
AXES = ("outer", "inner")
AMP_DEV = 262144
DEVICES = 256
TOTAL = AMP_DEV * DEVICES
WINDOW = 512
PITCH = 264
SPAN = 8 * PITCH


def reverse_bits(value, count):
    result = 0
    for bit in range(count):
        result = result + (value // 2**bit) % 2 * 2 ** (count - 1 - bit)
    return result


def scale_factor(sums_row):
    mean_square = jnp.sum(sums_row, axis=1, keepdims=True) / TOTAL
    return mean_square, lax.rsqrt(mean_square + 1e-06)


def exchange_kernel(
    x_hbm, placed_ref, late_ref, sums_ref,
    a_ref, high_ref, low_ref, bh_ref, bl_ref,
    send_ref, mid_a_ref, mid_b_ref, early_ref, zsum_ref, psum_ref,
    load_sem, send_sem, recv_sem,
):
    outer, inner = lax.axis_index("outer"), lax.axis_index("inner")
    y, c, x, z = outer // 2, outer % 2, inner // 8, inner % 8
    plane = outer * 4 + x
    z_slot, p_slot = reverse_bits(z, 3), reverse_bits(plane, 5)
    z_index = z % 2 * 4 + z // 2
    slot = z_slot * 32 + p_slot

    def z_peer(there):
        return (outer, x * 8 + there)

    def plane_peer(t):
        dx, dc, dy = t % 4, t // 4 % 2, t // 8
        there_outer, there_x = (y + dy) % 4 * 2 + (c + dc) % 2, (x + dx) % 4
        return (there_outer, there_x * 8 + z), there_outer * 4 + there_x

    loads = [
        [
            pltpu.make_async_copy(
                x_hbm.at[pl.ds(32 * top, 32), half],
                a_ref.at[half, reverse_bits(top, 3), pl.ds(0, 32)],
                load_sem.at[half, top],
            )
            for top in range(8)
        ]
        for half in range(2)
    ]
    for load in loads[0] + loads[1]:
        load.start()

    barrier = pltpu.get_barrier_semaphore()
    for d in range(1, 8):
        pl.semaphore_signal(barrier, inc=1, device_id=z_peer((z + d) % 8), device_id_type=MESH)

    def greet(t, _):
        pl.semaphore_signal(barrier, inc=1, device_id=plane_peer(t)[0], device_id_type=MESH)
        return 0

    lax.fori_loop(1, 32, greet, 0)

    lane = lax.broadcasted_iota(jnp.int32, (128, 128), 1)
    row = lax.broadcasted_iota(jnp.int32, (128, 128), 0)
    frequency = (row & 31) * 4 + (row >> 5)
    angle = ((frequency * lane) & 127).astype(jnp.float32) * (2.0 * math.pi / 128)
    for value, places in (
        (jnp.cos(angle) * WINDOW**-0.5, ((0, 0, 1.0), (1, 1, 1.0))),
        (jnp.sin(angle) * WINDOW**-0.5, ((1, 0, 1.0), (0, 1, -1.0))),
    ):
        high = value.astype(jnp.bfloat16)
        low = (value - high.astype(jnp.float32)).astype(jnp.bfloat16)
        for i, j, sign in places:
            high_ref[128 * i : 128 * i + 128, 128 * j : 128 * j + 128] = high * jnp.bfloat16(sign)
            low_ref[128 * i : 128 * i + 128, 128 * j : 128 * j + 128] = low * jnp.bfloat16(sign)
    lane = lax.broadcasted_iota(jnp.int32, (16, 128), 1)
    twiddles = []
    for g in (1, 2, 3):
        angle = (lane * g).astype(jnp.float32) * (2.0 * math.pi / WINDOW)
        twiddles.append((jnp.cos(angle), jnp.sin(angle)))

    step = 2.0 * math.pi * 2048 / TOTAL
    cos_step, sin_step = math.cos(step), math.sin(step)
    a_rows = a_ref.reshape(2 * SPAN, 128)
    zero = jnp.zeros((8, 128), jnp.float32)

    def spread_half(half, squares):
        for load in loads[half]:
            load.wait()

        def spread(turn, carry):
            squares, phase_real, phase_imag = carry
            h = 15 - turn
            middle = reverse_bits(h, 4)
            parts = [
                [
                    a_rows[pl.ds(half * SPAN + (middle + 16 * b) * 8 + q, 8, stride=PITCH), :]
                    for q in range(8)
                ]
                for b in range(2)
            ]
            for b in (1, 0):
                phase_real, phase_imag = (
                    phase_real * cos_step + phase_imag * sin_step + parts[b][0],
                    phase_imag * cos_step - phase_real * sin_step + parts[b][1],
                )
                for q in range(8):
                    squares = squares + parts[b][q] * parts[b][q]
            v = [jnp.concatenate([parts[0][q], parts[1][q]], 0) for q in range(8)]
            real, imag = v[0::2], v[1::2]
            s02r, s02i = real[0] + real[2], imag[0] + imag[2]
            d02r, d02i = real[0] - real[2], imag[0] - imag[2]
            s13r, s13i = real[1] + real[3], imag[1] + imag[3]
            d13r, d13i = real[1] - real[3], imag[1] - imag[3]
            u = [
                (s02r + s13r, s02i + s13i),
                (d02r - d13i, d02i + d13r),
                (s02r - s13r, s02i - s13i),
                (d02r + d13i, d02i - d13r),
            ]
            rows = pl.ds(pl.multiple_of(h * 16, 16), 16)
            for g in range(4):
                ur, ui = u[g]
                if g:
                    cosine, sine = twiddles[g - 1]
                    ur, ui = ur * cosine - ui * sine, ur * sine + ui * cosine
                for s, value in ((0, ur), (1, ui)):
                    high = value.astype(jnp.bfloat16)
                    low = (value - high.astype(jnp.float32)).astype(jnp.bfloat16)
                    bh_ref[g, rows, 128 * s : 128 * s + 128] = high
                    bl_ref[g, rows, 128 * s : 128 * s + 128] = low
            return squares, phase_real, phase_imag

        return lax.fori_loop(0, 16, spread, (squares, zero, zero))

    def transform(half, first):
        def body(f, _):
            g = first + f
            bh, bl = bh_ref[g], bl_ref[g]
            dims = (((1,), (1,)), ((), ()))
            out = (
                lax.dot_general(high_ref[...], bh, dims, preferred_element_type=jnp.float32)
                + lax.dot_general(high_ref[...], bl, dims, preferred_element_type=jnp.float32)
                + lax.dot_general(low_ref[...], bh, dims, preferred_element_type=jnp.float32)
            )
            for k in range(2):
                for s in range(2):
                    place = pl.ds(first // 2 * 1024 + f * 4 + k * 2 + s, 128, stride=8)
                    send_ref[half, place, :] = out[128 * s : 128 * s + 128, 128 * k : 128 * k + 128]
            return 0

        lax.fori_loop(0, 2, body, 0)

    def copy(peer, source, target, number):
        return pltpu.make_async_remote_copy(
            src_ref=source,
            dst_ref=target,
            send_sem=send_sem.at[number],
            recv_sem=recv_sem.at[number],
            device_id=peer,
            device_id_type=MESH,
        )

    def finish_recv(ref, number):
        copy(z_peer((z + 1) % 8), ref, ref, number).wait_recv()

    def finish_send(ref, number):
        copy(z_peer((z + 1) % 8), ref, ref, number).wait_send()

    early_send = send_ref.reshape(2, 8, 32, 8, 128).at[0]
    late_send = send_ref.reshape(2, 8, 32, 8, 128).at[1]

    squares, phase_real_0, phase_imag_0 = spread_half(0, zero)
    transform(0, 0)
    pl.semaphore_wait(barrier, 38)
    for parity in range(2):
        if parity:
            transform(0, 2)
        for high_part in range(4):
            there = 2 * high_part + parity

            @pl.when(there != z)
            def _():
                copy(z_peer(there), early_send.at[4 * parity + high_part], mid_a_ref.at[z_slot], 1).start()

    squares, phase_real_1, phase_imag_1 = spread_half(1, squares)
    transform(1, 0)
    transform(1, 2)

    def plane_bulk(source, target, number):
        def body(t, _):
            peer, there = plane_peer(t)
            copy(peer, source.at[:, there], target.at[:, p_slot], number).start()
            return 0

        lax.fori_loop(1, 32, body, 0)

    plane_bulk(late_send, mid_b_ref, 2)
    mid_a_ref[z_slot] = early_send[z_index]
    for i in range(8):
        mid_b_ref[i, p_slot] = late_send[i, plane]

    lane = lax.broadcasted_iota(jnp.int32, (8, 128), 1)
    sub = lax.broadcasted_iota(jnp.int32, (8, 128), 0)
    turned_real, turned_imag = zero, zero
    for half, phase_real, phase_imag in ((0, phase_real_0, phase_imag_0), (1, phase_real_1, phase_imag_1)):
        angle = (half * 65536 + sub * 256 + slot).astype(jnp.float32) * (2.0 * math.pi / TOTAL)
        cosine, sine = jnp.cos(angle), jnp.sin(angle)
        turned_real = turned_real + (phase_real * cosine + phase_imag * sine)
        turned_imag = turned_imag + (phase_imag * cosine - phase_real * sine)
    turned_real = jnp.where(lane == 1, turned_real, 0.0)
    turned_imag = jnp.where(lane == 1, turned_imag, 0.0)
    zsum_ref[z] = jnp.where(
        sub == 0,
        jnp.sum(squares, 0, keepdims=True),
        jnp.where(
            sub == 1,
            jnp.sum(turned_real, 0, keepdims=True),
            jnp.where(sub == 2, jnp.sum(turned_imag, 0, keepdims=True), 0.0),
        ),
    )
    for d in range(1, 8):
        copy(z_peer((z + d) % 8), zsum_ref.at[z], zsum_ref.at[z], 0).start()

    finish_recv(mid_b_ref.at[:, pl.ds(0, 31)], 2)
    for d in (4, 3, 5, 2, 6, 1, 7):
        there = (z + d) % 8
        copy(z_peer(there), mid_b_ref.at[there % 2 * 4 + there // 2], late_ref.at[z_slot], 4).start()
    late_ref[z_slot] = mid_b_ref[z_index]

    finish_recv(zsum_ref.at[pl.ds(0, 7)], 0)
    total = zsum_ref[0]
    for i in range(1, 8):
        total = total + zsum_ref[i]
    psum_ref[plane] = total

    def plane_sums(t, _):
        copy(plane_peer(t)[0], psum_ref.at[plane], psum_ref.at[plane], 3).start()
        return 0

    lax.fori_loop(1, 32, plane_sums, 0)

    finish_recv(mid_a_ref.at[pl.ds(0, 7)], 1)
    plane_bulk(mid_a_ref, early_ref, 5)
    for i in range(8):
        early_ref[i, p_slot] = mid_a_ref[i, plane]

    finish_recv(psum_ref.at[pl.ds(0, 31)], 3)
    total = psum_ref[0]
    for i in range(1, 32):
        total = total + psum_ref[i]
    sums_ref[...] = total
    factor = scale_factor(total[0:1])[1]

    finish_recv(early_ref.at[:, pl.ds(0, 31)], 5)
    place_rows(early_ref.reshape(2048, 128), placed_ref, factor)

    finish_recv(late_ref.at[pl.ds(0, 7)], 4)
    finish_send(zsum_ref.at[pl.ds(0, 7)], 0)
    finish_send(mid_a_ref.at[pl.ds(0, 7)], 1)
    finish_send(mid_b_ref.at[:, pl.ds(0, 31)], 2)
    finish_send(psum_ref.at[pl.ds(0, 31)], 3)
    finish_send(mid_b_ref.at[pl.ds(0, 7)], 4)
    finish_send(early_ref.at[:, pl.ds(0, 31)], 5)


def place_rows(source, target, factor):
    def body(part, _):
        place_part(source, target, factor, part)
        return 0

    lax.fori_loop(0, 4, body, 0)


def place_part(source, target, factor, part):
    for s in range(2):
        for d in range(2):
            block = source[pl.ds(d * 1024 + part * 2 + s, 128, stride=8), :]
            target[pl.ds(part * 512 + d * 2 + s, 128, stride=4), :] = block.T * factor


def place_kernel(placed_ref, late_ref, sums_ref, out_hbm, checks_ref, buffer_ref, sems):
    copies = []

    def move(source, first, size, number):
        copies.append(pltpu.make_async_copy(source, out_hbm.at[pl.ds(first, size)], sems.at[number]))
        copies[-1].start()

    for f in range(2):
        move(placed_ref.at[pl.ds(f * 1024, 1024)], f * 2048, 1024, f)
    mean_square, factor = scale_factor(sums_ref[pl.ds(0, 1), :])
    for part in range(4):
        place_part(late_ref, buffer_ref, factor, part)
        first = part // 2 * 2048 + 1024 + part % 2 * 512
        move(buffer_ref.at[pl.ds(part * 512, 512)], first, 512, 2 + part)
    scale = factor * (math.sqrt(WINDOW) / math.sqrt(TOTAL))
    checks_ref[0] = mean_square[0, 0]
    for i in (1, 2):
        value = jnp.sum(sums_ref[pl.ds(i, 1), :], axis=1, keepdims=True) * scale
        checks_ref[i] = value[0, 0]
    for moved in copies:
        moved.wait()


def per_device(amplitudes):
    rows = amplitudes.reshape(2, 2048, 128).transpose(1, 0, 2).reshape(256, 2, 8, 128)
    vmem = pl.BlockSpec(memory_space=pltpu.VMEM)
    hbm = pl.BlockSpec(memory_space=pltpu.HBM)
    f32, bf16 = jnp.float32, jnp.bfloat16
    placed, late, sums = pl.pallas_call(
        exchange_kernel,
        out_shape=(
            jax.ShapeDtypeStruct((2048, 128), f32),
            jax.ShapeDtypeStruct((8, 32, 8, 128), f32),
            jax.ShapeDtypeStruct((8, 128), f32),
        ),
        in_specs=[hbm],
        out_specs=(vmem, vmem, vmem),
        scratch_shapes=[
            pltpu.VMEM((2, 8, 33, 8, 128), f32),
            pltpu.VMEM((256, 256), bf16),
            pltpu.VMEM((256, 256), bf16),
            pltpu.VMEM((4, 256, 256), bf16),
            pltpu.VMEM((4, 256, 256), bf16),
            pltpu.VMEM((2, 2048, 128), f32),
            pltpu.VMEM((8, 32, 8, 128), f32),
            pltpu.VMEM((8, 32, 8, 128), f32),
            pltpu.VMEM((8, 32, 8, 128), f32),
            pltpu.VMEM((8, 8, 128), f32),
            pltpu.VMEM((32, 8, 128), f32),
            pltpu.SemaphoreType.DMA((2, 8)),
            pltpu.SemaphoreType.DMA((6,)),
            pltpu.SemaphoreType.DMA((6,)),
        ],
        compiler_params=pltpu.CompilerParams(
            collective_id=1, has_side_effects=True, vmem_limit_bytes=51 * 1024 * 1024
        ),
    )(rows)
    out, checks = pl.pallas_call(
        place_kernel,
        out_shape=(
            jax.ShapeDtypeStruct((4096, 128), f32),
            jax.ShapeDtypeStruct((3,), f32),
        ),
        in_specs=[vmem, vmem, vmem],
        out_specs=(hbm, pl.BlockSpec(memory_space=pltpu.SMEM)),
        scratch_shapes=[pltpu.VMEM((2048, 128), f32), pltpu.SemaphoreType.DMA((6,))],
        compiler_params=pltpu.CompilerParams(vmem_limit_bytes=16 * 1024 * 1024),
    )(placed, late.reshape(2048, 128), sums)
    transformed = out.reshape(2048, 2, 128).transpose(1, 0, 2).reshape(2, AMP_DEV)
    return transformed, checks


def solution(mesh):
    return jax.shard_map(
        per_device,
        mesh=mesh,
        in_specs=(P(None, AXES),),
        out_specs=(P(None, AXES), P()),
        check_vma=False,
    )
```

time: 67 us -> 62.6 us (0.934)
  local copies, waits for them, and re-layouts: 4.08 us -> 0 us
    unnamed x8 -> x0, local copies, waits for them, and re-layouts: 4.08 us -> none
where the time goes in v3:
time: 62.6 us; the launch traced here: 62.5 us
  Pallas kernels  61.9 us (99%)
  between operations  0.64 us (1%)
    pallas_call x1, Pallas kernels, per_device(): pl.pallas_call(exchange_kernel, out_shape=(jax.ShapeDtypeStruct((2048, 12...  60 us
    pallas_call x1, Pallas kernels, per_device(): pl.pallas_call(place_kernel, out_shape=(jax.ShapeDtypeStruct((4096, 128),...  1.88 us

profile of v3, /device:TPU:1, one launch (start us, length us, event | category | flops | bytes accessed | tf_op | source)
XLA Modules:
  0.0 62.5 jit_solution(10353334436389994616)
XLA Ops:
  0.6 60.0 %shard_map.30 = (f32[2048,128]{1,0:T(8,128)S(1)}, f32[8,32,8,128]{3,2,1,0:T(8,128)S(1)}, f32[8,128]{1,0:T(8,128)S(1)}) custom-call(f32[256,2,8,128]{3,2,1,0:T(8,128)} %bitcast.12), custom_call_target="tpu_custom_call" | custom-call | tf_op jit(solution)/shard_map/pallas_call | solution.py:324
  60.7 1.9 %shard_map.31 = (f32[4096,128]{1,0:T(8,128)}, f32[3]{0:T(128)}) custom-call(f32[2048,128]{1,0:T(8,128)S(1)} %get-tuple-element.7.placed_ref, f32[2048,128]{1,0:T(8,128)S(1)} %bitcast.11, f32[8,128]{1,0:T(8,128)S(1)} %get-tuple-element.9.sums_ref), custom_call_target="tpu_custom_call" | custom-call | tf_op jit(solution)/shard_map/pallas_call | solution.py:353

commit v4 on v3

--- a/solution.py
+++ b/solution.py
@@ -24,8 +24,8 @@
     return result
 
 
-def scale_factor(sums_row):
-    mean_square = jnp.sum(sums_row, axis=1, keepdims=True) / TOTAL
+def scale_factor(squares):
+    mean_square = squares / TOTAL
     return mean_square, lax.rsqrt(mean_square + 1e-06)
 
 
@@ -33,7 +33,7 @@
     x_hbm, placed_ref, late_ref, sums_ref,
     a_ref, high_ref, low_ref, bh_ref, bl_ref,
     send_ref, mid_a_ref, mid_b_ref, early_ref, zsum_ref, psum_ref,
-    load_sem, send_sem, recv_sem,
+    load_sem, send_sem, recv_sem, round_sem,
 ):
     outer, inner = lax.axis_index("outer"), lax.axis_index("inner")
     y, c, x, z = outer // 2, outer % 2, inner // 8, inner % 8
@@ -46,7 +46,7 @@
         return (outer, x * 8 + there)
 
     def plane_peer(t):
-        dx, dc, dy = t % 4, t // 4 % 2, t // 8
+        dx, dy, dc = t % 4, (t % 4 + t // 4) % 4, (t + t // 16) % 2
         there_outer, there_x = (y + dy) % 4 * 2 + (c + dc) % 2, (x + dx) % 4
         return (there_outer, there_x * 8 + z), there_outer * 4 + there_x
 
@@ -72,7 +72,9 @@
         pl.semaphore_signal(barrier, inc=1, device_id=plane_peer(t)[0], device_id_type=MESH)
         return 0
 
-    lax.fori_loop(1, 32, greet, 0)
+    @pl.when(z == 0)
+    def _():
+        lax.fori_loop(1, 32, greet, 0)
 
     lane = lax.broadcasted_iota(jnp.int32, (128, 128), 1)
     row = lax.broadcasted_iota(jnp.int32, (128, 128), 0)
@@ -186,20 +188,36 @@
 
     squares, phase_real_0, phase_imag_0 = spread_half(0, zero)
     transform(0, 0)
-    pl.semaphore_wait(barrier, 38)
-    for parity in range(2):
-        if parity:
-            transform(0, 2)
-        for high_part in range(4):
-            there = 2 * high_part + parity
-
-            @pl.when(there != z)
-            def _():
-                copy(z_peer(there), early_send.at[4 * parity + high_part], mid_a_ref.at[z_slot], 1).start()
+    transform(0, 2)
+    pl.semaphore_wait(barrier, 7 + jnp.where(z == 0, 31, 0))
+
+    def early_z(there):
+        copy(z_peer(there), early_send.at[there % 2 * 4 + there // 2], mid_a_ref.at[z_slot], 1).start()
+
+    for d in (4, 3, 5, 2, 6, 1, 7):
+        early_z((z + d) % 8)
+
+    def line_ready(t, _):
+        pl.semaphore_signal(round_sem.at[0], inc=1, device_id=plane_peer(t)[0], device_id_type=MESH)
+        return 0
+
+    @pl.when(z == 0)
+    def _():
+        lax.fori_loop(1, 32, line_ready, 0)
 
     squares, phase_real_1, phase_imag_1 = spread_half(1, squares)
     transform(1, 0)
     transform(1, 2)
+
+    @pl.when(z == 0)
+    def _():
+        pl.semaphore_wait(round_sem.at[0], 31)
+        for there in range(1, 8):
+            pl.semaphore_signal(round_sem.at[1], inc=1, device_id=z_peer(there), device_id_type=MESH)
+
+    @pl.when(z != 0)
+    def _():
+        pl.semaphore_wait(round_sem.at[1], 1)
 
     def plane_bulk(source, target, number):
         def body(t, _):
@@ -214,7 +232,7 @@
     for i in range(8):
         mid_b_ref[i, p_slot] = late_send[i, plane]
 
-    lane = lax.broadcasted_iota(jnp.int32, (8, 128), 1)
+    column = lax.broadcasted_iota(jnp.int32, (8, 128), 1)
     sub = lax.broadcasted_iota(jnp.int32, (8, 128), 0)
     turned_real, turned_imag = zero, zero
     for half, phase_real, phase_imag in ((0, phase_real_0, phase_imag_0), (1, phase_real_1, phase_imag_1)):
@@ -222,24 +240,24 @@
         cosine, sine = jnp.cos(angle), jnp.sin(angle)
         turned_real = turned_real + (phase_real * cosine + phase_imag * sine)
         turned_imag = turned_imag + (phase_imag * cosine - phase_real * sine)
-    turned_real = jnp.where(lane == 1, turned_real, 0.0)
-    turned_imag = jnp.where(lane == 1, turned_imag, 0.0)
-    zsum_ref[z] = jnp.where(
-        sub == 0,
-        jnp.sum(squares, 0, keepdims=True),
-        jnp.where(
-            sub == 1,
-            jnp.sum(turned_real, 0, keepdims=True),
-            jnp.where(sub == 2, jnp.sum(turned_imag, 0, keepdims=True), 0.0),
-        ),
-    )
+    lane = lax.broadcasted_iota(jnp.int32, (1, 128), 1)
+    row = jnp.zeros((1, 128), jnp.float32)
+    for i, value in enumerate((
+        squares, jnp.where(column == 1, turned_real, 0.0), jnp.where(column == 1, turned_imag, 0.0),
+    )):
+        summed = jnp.sum(jnp.sum(value, 0, keepdims=True), 1, keepdims=True)
+        row = jnp.where(lane == i, summed, row)
+    zsum_ref[z] = row
     for d in range(1, 8):
         copy(z_peer((z + d) % 8), zsum_ref.at[z], zsum_ref.at[z], 0).start()
 
     finish_recv(mid_b_ref.at[:, pl.ds(0, 31)], 2)
+    def late_z(there):
+        copy(z_peer(there), mid_b_ref.at[there % 2 * 4 + there // 2], late_ref.at[z_slot], 4).start()
+
     for d in (4, 3, 5, 2, 6, 1, 7):
-        there = (z + d) % 8
-        copy(z_peer(there), mid_b_ref.at[there % 2 * 4 + there // 2], late_ref.at[z_slot], 4).start()
+        late_z((z + d) % 8)
+
     late_ref[z_slot] = mid_b_ref[z_index]
 
     finish_recv(zsum_ref.at[pl.ds(0, 7)], 0)
@@ -264,7 +282,7 @@
     for i in range(1, 32):
         total = total + psum_ref[i]
     sums_ref[...] = total
-    factor = scale_factor(total[0:1])[1]
+    factor = scale_factor(total[:, 0:1])[1]
 
     finish_recv(early_ref.at[:, pl.ds(0, 31)], 5)
     place_rows(early_ref.reshape(2048, 128), placed_ref, factor)
@@ -302,7 +320,8 @@
 
     for f in range(2):
         move(placed_ref.at[pl.ds(f * 1024, 1024)], f * 2048, 1024, f)
-    mean_square, factor = scale_factor(sums_ref[pl.ds(0, 1), :])
+    sums = sums_ref[...]
+    mean_square, factor = scale_factor(sums[:, 0:1])
     for part in range(4):
         place_part(late_ref, buffer_ref, factor, part)
         first = part // 2 * 2048 + 1024 + part % 2 * 512
@@ -310,8 +329,7 @@
     scale = factor * (math.sqrt(WINDOW) / math.sqrt(TOTAL))
     checks_ref[0] = mean_square[0, 0]
     for i in (1, 2):
-        value = jnp.sum(sums_ref[pl.ds(i, 1), :], axis=1, keepdims=True) * scale
-        checks_ref[i] = value[0, 0]
+        checks_ref[i] = (sums[:, i : i + 1] * scale)[0, 0]
     for moved in copies:
         moved.wait()
 
@@ -326,7 +344,7 @@
         out_shape=(
             jax.ShapeDtypeStruct((2048, 128), f32),
             jax.ShapeDtypeStruct((8, 32, 8, 128), f32),
-            jax.ShapeDtypeStruct((8, 128), f32),
+            jax.ShapeDtypeStruct((1, 128), f32),
         ),
         in_specs=[hbm],
         out_specs=(vmem, vmem, vmem),
@@ -340,11 +358,12 @@
             pltpu.VMEM((8, 32, 8, 128), f32),
             pltpu.VMEM((8, 32, 8, 128), f32),
             pltpu.VMEM((8, 32, 8, 128), f32),
-            pltpu.VMEM((8, 8, 128), f32),
-            pltpu.VMEM((32, 8, 128), f32),
+            pltpu.VMEM((8, 1, 128), f32),
+            pltpu.VMEM((32, 1, 128), f32),
             pltpu.SemaphoreType.DMA((2, 8)),
             pltpu.SemaphoreType.DMA((6,)),
             pltpu.SemaphoreType.DMA((6,)),
+            pltpu.SemaphoreType.REGULAR((2,)),
         ],
         compiler_params=pltpu.CompilerParams(
             collective_id=1, has_side_effects=True, vmem_limit_bytes=51 * 1024 * 1024

time: 62.6 us -> 59 us (0.942)
  Pallas kernels: 61.9 us -> 58.3 us
    pallas_call x1, Pallas kernels: 60 us -> 56.3 us  [per_device(): pl.pallas_call(exchange_kernel, out_shape=(jax.ShapeDtypeStruct((2048, 12...]
where the time goes in v4:
time: 59 us; the launch traced here: 58.9 us
  Pallas kernels  58.3 us (99%)
  between operations  0.64 us (1%)
    pallas_call x1, Pallas kernels, per_device(): pl.pallas_call(exchange_kernel, out_shape=(jax.ShapeDtypeStruct((2048, 12...  56.3 us
    pallas_call x1, Pallas kernels, per_device(): pl.pallas_call(place_kernel, out_shape=(jax.ShapeDtypeStruct((4096, 128),...  1.92 us

profile of v4, /device:TPU:1, one launch (start us, length us, event | category | flops | bytes accessed | tf_op | source)
XLA Modules:
  0.0 58.9 jit_solution(3443974794968026730)
XLA Ops:
  0.6 56.3 %shard_map.30 = (f32[2048,128]{1,0:T(8,128)S(1)}, f32[8,32,8,128]{3,2,1,0:T(8,128)S(1)}, f32[1,128]{1,0:T(1,128)S(1)}) custom-call(f32[256,2,8,128]{3,2,1,0:T(8,128)} %bitcast.12), custom_call_target="tpu_custom_call" | custom-call | tf_op jit(solution)/shard_map/pallas_call | solution.py:342
  57.0 1.9 %shard_map.31 = (f32[4096,128]{1,0:T(8,128)}, f32[3]{0:T(128)}) custom-call(f32[2048,128]{1,0:T(8,128)S(1)} %get-tuple-element.7.placed_ref, f32[2048,128]{1,0:T(8,128)S(1)} %bitcast.11, f32[1,128]{1,0:T(1,128)S(1)} %get-tuple-element.9.sums_ref), custom_call_target="tpu_custom_call" | custom-call | tf_op jit(solution)/shard_map/pallas_call | solution.py:372

commit v5 on v4

--- a/solution.py
+++ b/solution.py
@@ -35,21 +35,6 @@
     send_ref, mid_a_ref, mid_b_ref, early_ref, zsum_ref, psum_ref,
     load_sem, send_sem, recv_sem, round_sem,
 ):
-    outer, inner = lax.axis_index("outer"), lax.axis_index("inner")
-    y, c, x, z = outer // 2, outer % 2, inner // 8, inner % 8
-    plane = outer * 4 + x
-    z_slot, p_slot = reverse_bits(z, 3), reverse_bits(plane, 5)
-    z_index = z % 2 * 4 + z // 2
-    slot = z_slot * 32 + p_slot
-
-    def z_peer(there):
-        return (outer, x * 8 + there)
-
-    def plane_peer(t):
-        dx, dy, dc = t % 4, (t % 4 + t // 4) % 4, (t + t // 16) % 2
-        there_outer, there_x = (y + dy) % 4 * 2 + (c + dc) % 2, (x + dx) % 4
-        return (there_outer, there_x * 8 + z), there_outer * 4 + there_x
-
     loads = [
         [
             pltpu.make_async_copy(
@@ -61,8 +46,23 @@
         ]
         for half in range(2)
     ]
-    for load in loads[0] + loads[1]:
+    for load in loads[0]:
         load.start()
+
+    outer, inner = lax.axis_index("outer"), lax.axis_index("inner")
+    y, c, x, z = outer // 2, outer % 2, inner // 8, inner % 8
+    plane = outer * 4 + x
+    z_slot, p_slot = reverse_bits(z, 3), reverse_bits(plane, 5)
+    z_index = z % 2 * 4 + z // 2
+    slot = z_slot * 32 + p_slot
+
+    def z_peer(there):
+        return (outer, x * 8 + there)
+
+    def plane_peer(t):
+        dx, dy, dc = t % 4, (t % 4 + t // 4) % 4, (t + t // 16) % 2
+        there_outer, there_x = (y + dy) % 4 * 2 + (c + dc) % 2, (x + dx) % 4
+        return (there_outer, there_x * 8 + z), there_outer * 4 + there_x
 
     barrier = pltpu.get_barrier_semaphore()
     for d in range(1, 8):
@@ -103,6 +103,9 @@
     def spread_half(half, squares):
         for load in loads[half]:
             load.wait()
+        if half == 0:
+            for load in loads[1]:
+                load.start()
 
         def spread(turn, carry):
             squares, phase_real, phase_imag = carry
@@ -150,9 +153,8 @@
         return lax.fori_loop(0, 16, spread, (squares, zero, zero))
 
     def transform(half, first):
-        def body(f, _):
-            g = first + f
-            bh, bl = bh_ref[g], bl_ref[g]
+        for f in range(2):
+            bh, bl = bh_ref[first + f], bl_ref[first + f]
             dims = (((1,), (1,)), ((), ()))
             out = (
                 lax.dot_general(high_ref[...], bh, dims, preferred_element_type=jnp.float32)
@@ -163,9 +165,6 @@
                 for s in range(2):
                     place = pl.ds(first // 2 * 1024 + f * 4 + k * 2 + s, 128, stride=8)
                     send_ref[half, place, :] = out[128 * s : 128 * s + 128, 128 * k : 128 * k + 128]
-            return 0
-
-        lax.fori_loop(0, 2, body, 0)
 
     def copy(peer, source, target, number):
         return pltpu.make_async_remote_copy(
@@ -187,15 +186,25 @@
     late_send = send_ref.reshape(2, 8, 32, 8, 128).at[1]
 
     squares, phase_real_0, phase_imag_0 = spread_half(0, zero)
-    transform(0, 0)
-    transform(0, 2)
-    pl.semaphore_wait(barrier, 7 + jnp.where(z == 0, 31, 0))
-
     def early_z(there):
         copy(z_peer(there), early_send.at[there % 2 * 4 + there // 2], mid_a_ref.at[z_slot], 1).start()
 
-    for d in (4, 3, 5, 2, 6, 1, 7):
-        early_z((z + d) % 8)
+    def early_sends(odd):
+        @pl.when((z + odd) % 2 == 0)
+        def _():
+            for d in (4, 2, 6):
+                early_z((z + d) % 8)
+
+        @pl.when((z + odd) % 2 == 1)
+        def _():
+            for d in (3, 5, 1, 7):
+                early_z((z + d) % 8)
+
+    transform(0, 0)
+    pl.semaphore_wait(barrier, 7 + jnp.where(z == 0, 31, 0))
+    early_sends(0)
+    transform(0, 2)
+    early_sends(1)
 
     def line_ready(t, _):
         pl.semaphore_signal(round_sem.at[0], inc=1, device_id=plane_peer(t)[0], device_id_type=MESH)
@@ -208,29 +217,6 @@
     squares, phase_real_1, phase_imag_1 = spread_half(1, squares)
     transform(1, 0)
     transform(1, 2)
-
-    @pl.when(z == 0)
-    def _():
-        pl.semaphore_wait(round_sem.at[0], 31)
-        for there in range(1, 8):
-            pl.semaphore_signal(round_sem.at[1], inc=1, device_id=z_peer(there), device_id_type=MESH)
-
-    @pl.when(z != 0)
-    def _():
-        pl.semaphore_wait(round_sem.at[1], 1)
-
-    def plane_bulk(source, target, number):
-        def body(t, _):
-            peer, there = plane_peer(t)
-            copy(peer, source.at[:, there], target.at[:, p_slot], number).start()
-            return 0
-
-        lax.fori_loop(1, 32, body, 0)
-
-    plane_bulk(late_send, mid_b_ref, 2)
-    mid_a_ref[z_slot] = early_send[z_index]
-    for i in range(8):
-        mid_b_ref[i, p_slot] = late_send[i, plane]
 
     column = lax.broadcasted_iota(jnp.int32, (8, 128), 1)
     sub = lax.broadcasted_iota(jnp.int32, (8, 128), 0)
@@ -247,40 +233,63 @@
     )):
         summed = jnp.sum(jnp.sum(value, 0, keepdims=True), 1, keepdims=True)
         row = jnp.where(lane == i, summed, row)
-    zsum_ref[z] = row
+    psum_ref[plane] = row
+
+    @pl.when(z == 0)
+    def _():
+        pl.semaphore_wait(round_sem.at[0], 31)
+        for there in range(1, 8):
+            pl.semaphore_signal(round_sem.at[1], inc=1, device_id=z_peer(there), device_id_type=MESH)
+
+    @pl.when(z != 0)
+    def _():
+        pl.semaphore_wait(round_sem.at[1], 1)
+
+    def plane_bulk(source, target, number):
+        def body(t, _):
+            peer, there = plane_peer(t)
+            copy(peer, source.at[:, there], target.at[:, p_slot], number).start()
+            return 0
+
+        lax.fori_loop(1, 32, body, 0)
+
+    def plane_sums(t, _):
+        copy(plane_peer(t)[0], psum_ref.at[plane], psum_ref.at[plane], 3).start()
+        return 0
+
+    lax.fori_loop(1, 32, plane_sums, 0)
+    plane_bulk(late_send, mid_b_ref, 2)
+    mid_a_ref[z_slot] = early_send[z_index]
+    for i in range(8):
+        mid_b_ref[i, p_slot] = late_send[i, plane]
+
+    finish_recv(psum_ref.at[pl.ds(0, 31)], 3)
+    total = psum_ref[0]
+    for i in range(1, 32):
+        total = total + psum_ref[i]
+    zsum_ref[z] = total
     for d in range(1, 8):
         copy(z_peer((z + d) % 8), zsum_ref.at[z], zsum_ref.at[z], 0).start()
 
     finish_recv(mid_b_ref.at[:, pl.ds(0, 31)], 2)
+
     def late_z(there):
         copy(z_peer(there), mid_b_ref.at[there % 2 * 4 + there // 2], late_ref.at[z_slot], 4).start()
 
-    for d in (4, 3, 5, 2, 6, 1, 7):
-        late_z((z + d) % 8)
+    for there in (0, 1, 2, 3, 4, 5, 6, 7):
+        pl.when(there != z)(lambda there=there: late_z(there))
 
     late_ref[z_slot] = mid_b_ref[z_index]
+
+    finish_recv(mid_a_ref.at[pl.ds(0, 7)], 1)
+    plane_bulk(mid_a_ref, early_ref, 5)
+    for i in range(8):
+        early_ref[i, p_slot] = mid_a_ref[i, plane]
 
     finish_recv(zsum_ref.at[pl.ds(0, 7)], 0)
     total = zsum_ref[0]
     for i in range(1, 8):
         total = total + zsum_ref[i]
-    psum_ref[plane] = total
-
-    def plane_sums(t, _):
-        copy(plane_peer(t)[0], psum_ref.at[plane], psum_ref.at[plane], 3).start()
-        return 0
-
-    lax.fori_loop(1, 32, plane_sums, 0)
-
-    finish_recv(mid_a_ref.at[pl.ds(0, 7)], 1)
-    plane_bulk(mid_a_ref, early_ref, 5)
-    for i in range(8):
-        early_ref[i, p_slot] = mid_a_ref[i, plane]
-
-    finish_recv(psum_ref.at[pl.ds(0, 31)], 3)
-    total = psum_ref[0]
-    for i in range(1, 32):
-        total = total + psum_ref[i]
     sums_ref[...] = total
     factor = scale_factor(total[:, 0:1])[1]
 

time: 59 us -> 56.8 us (0.963)
  the two profiles are of different devices: /device:TPU:1 before, /device:TPU:64 now
where the time goes in v5:
time: 56.8 us; the launch traced here: 56.7 us
  Pallas kernels  56.1 us (99%)
  between operations  0.64 us (1%)
    pallas_call x1, Pallas kernels, per_device(): pl.pallas_call(exchange_kernel, out_shape=(jax.ShapeDtypeStruct((2048, 12...  54.1 us
    pallas_call x1, Pallas kernels, per_device(): pl.pallas_call(place_kernel, out_shape=(jax.ShapeDtypeStruct((4096, 128),...  1.92 us

profile of v5, /device:TPU:64, one launch (start us, length us, event | category | flops | bytes accessed | tf_op | source)
XLA Modules:
  0.0 56.7 jit_solution(14464730765097234452)
XLA Ops:
  0.6 54.1 %shard_map.30 = (f32[2048,128]{1,0:T(8,128)S(1)}, f32[8,32,8,128]{3,2,1,0:T(8,128)S(1)}, f32[1,128]{1,0:T(1,128)S(1)}) custom-call(f32[256,2,8,128]{3,2,1,0:T(8,128)} %bitcast.12), custom_call_target="tpu_custom_call" | custom-call | tf_op jit(solution)/shard_map/pallas_call | solution.py:351
  54.8 1.9 %shard_map.31 = (f32[4096,128]{1,0:T(8,128)}, f32[3]{0:T(128)}) custom-call(f32[2048,128]{1,0:T(8,128)S(1)} %get-tuple-element.7.placed_ref, f32[2048,128]{1,0:T(8,128)S(1)} %bitcast.11, f32[1,128]{1,0:T(1,128)S(1)} %get-tuple-element.9.sums_ref), custom_call_target="tpu_custom_call" | custom-call | tf_op jit(solution)/shard_map/pallas_call | solution.py:381

commit v6 on v5

--- a/solution.py
+++ b/solution.py
@@ -320,7 +320,7 @@
             target[pl.ds(part * 512 + d * 2 + s, 128, stride=4), :] = block.T * factor
 
 
-def place_kernel(placed_ref, late_ref, sums_ref, out_hbm, checks_ref, buffer_ref, sems):
+def place_kernel(placed_ref, late_ref, sums_ref, out_hbm, checks_hbm, buffer_ref, checks_ref, sems):
     copies = []
 
     def move(source, first, size, number):
@@ -331,14 +331,16 @@
         move(placed_ref.at[pl.ds(f * 1024, 1024)], f * 2048, 1024, f)
     sums = sums_ref[...]
     mean_square, factor = scale_factor(sums[:, 0:1])
+    scale = factor * (math.sqrt(WINDOW) / math.sqrt(TOTAL))
+    checks_ref[0] = mean_square[0, 0]
+    for i in (1, 2):
+        checks_ref[i] = (sums[:, i : i + 1] * scale)[0, 0]
+    copies.append(pltpu.make_async_copy(checks_ref, checks_hbm, sems.at[6]))
+    copies[-1].start()
     for part in range(4):
         place_part(late_ref, buffer_ref, factor, part)
         first = part // 2 * 2048 + 1024 + part % 2 * 512
         move(buffer_ref.at[pl.ds(part * 512, 512)], first, 512, 2 + part)
-    scale = factor * (math.sqrt(WINDOW) / math.sqrt(TOTAL))
-    checks_ref[0] = mean_square[0, 0]
-    for i in (1, 2):
-        checks_ref[i] = (sums[:, i : i + 1] * scale)[0, 0]
     for moved in copies:
         moved.wait()
 
@@ -385,8 +387,12 @@
             jax.ShapeDtypeStruct((3,), f32),
         ),
         in_specs=[vmem, vmem, vmem],
-        out_specs=(hbm, pl.BlockSpec(memory_space=pltpu.SMEM)),
-        scratch_shapes=[pltpu.VMEM((2048, 128), f32), pltpu.SemaphoreType.DMA((6,))],
+        out_specs=(hbm, hbm),
+        scratch_shapes=[
+            pltpu.VMEM((2048, 128), f32),
+            pltpu.SMEM((3,), f32),
+            pltpu.SemaphoreType.DMA((7,)),
+        ],
         compiler_params=pltpu.CompilerParams(vmem_limit_bytes=16 * 1024 * 1024),
     )(placed, late.reshape(2048, 128), sums)
     transformed = out.reshape(2048, 2, 128).transpose(1, 0, 2).reshape(2, AMP_DEV)

time: 56.8 us -> 56.3 us (level)
  Pallas kernels: 56.1 us -> 55.5 us
where the time goes in v6:
time: 56.3 us; the launch traced here: 56.2 us
  Pallas kernels  55.5 us (99%)
  between operations  0.64 us (1%)
    pallas_call x1, Pallas kernels, per_device(): pl.pallas_call(exchange_kernel, out_shape=(jax.ShapeDtypeStruct((2048, 12...  54.1 us
    pallas_call x1, Pallas kernels, per_device(): pl.pallas_call(place_kernel, out_shape=(jax.ShapeDtypeStruct((4096, 128),...  1.37 us

profile of v6, /device:TPU:64, one launch (start us, length us, event | category | flops | bytes accessed | tf_op | source)
XLA Modules:
  0.0 56.2 jit_solution(4763918822242320003)
XLA Ops:
  0.6 54.1 %shard_map.30 = (f32[2048,128]{1,0:T(8,128)S(1)}, f32[8,32,8,128]{3,2,1,0:T(8,128)S(1)}, f32[1,128]{1,0:T(1,128)S(1)}) custom-call(f32[256,2,8,128]{3,2,1,0:T(8,128)} %bitcast.12), custom_call_target="tpu_custom_call" | custom-call | tf_op jit(solution)/shard_map/pallas_call | solution.py:353
  54.8 1.4 %shard_map.31 = (f32[4096,128]{1,0:T(8,128)}, f32[3]{0:T(128)}) custom-call(f32[2048,128]{1,0:T(8,128)S(1)} %get-tuple-element.7.placed_ref, f32[2048,128]{1,0:T(8,128)S(1)} %bitcast.11, f32[1,128]{1,0:T(1,128)S(1)} %get-tuple-element.9.sums_ref), custom_call_target="tpu_custom_call" | custom-call | tf_op jit(solution)/shard_map/pallas_call | solution.py:383

commit v7 on v6

--- a/solution.py
+++ b/solution.py
@@ -183,7 +183,7 @@
         copy(z_peer((z + 1) % 8), ref, ref, number).wait_send()
 
     early_send = send_ref.reshape(2, 8, 32, 8, 128).at[0]
-    late_send = send_ref.reshape(2, 8, 32, 8, 128).at[1]
+    late_send = send_ref.reshape(2, 2, 4, 32, 8, 128).at[1]
 
     squares, phase_real_0, phase_imag_0 = spread_half(0, zero)
     def early_z(there):
@@ -258,10 +258,21 @@
         return 0
 
     lax.fori_loop(1, 32, plane_sums, 0)
-    plane_bulk(late_send, mid_b_ref, 2)
+
+    def late_bulk(part):
+        def body(t, _):
+            peer, there = plane_peer(t)
+            source = late_send.at[:, pl.ds(2 * part, 2), there]
+            copy(peer, source, mid_b_ref.at[:, pl.ds(2 * part, 2), p_slot], 2 + 4 * part).start()
+            return 0
+
+        lax.fori_loop(1, 32, body, 0)
+
+    late_bulk(0)
+    late_bulk(1)
     mid_a_ref[z_slot] = early_send[z_index]
     for i in range(8):
-        mid_b_ref[i, p_slot] = late_send[i, plane]
+        mid_b_ref[i // 4, i % 4, p_slot] = late_send[i // 4, i % 4, plane]
 
     finish_recv(psum_ref.at[pl.ds(0, 31)], 3)
     total = psum_ref[0]
@@ -271,15 +282,15 @@
     for d in range(1, 8):
         copy(z_peer((z + d) % 8), zsum_ref.at[z], zsum_ref.at[z], 0).start()
 
-    finish_recv(mid_b_ref.at[:, pl.ds(0, 31)], 2)
-
     def late_z(there):
-        copy(z_peer(there), mid_b_ref.at[there % 2 * 4 + there // 2], late_ref.at[z_slot], 4).start()
-
-    for there in (0, 1, 2, 3, 4, 5, 6, 7):
-        pl.when(there != z)(lambda there=there: late_z(there))
-
-    late_ref[z_slot] = mid_b_ref[z_index]
+        copy(z_peer(there), mid_b_ref.at[there % 2, there // 2], late_ref.at[z_slot], 4).start()
+
+    for part in range(2):
+        finish_recv(mid_b_ref.at[:, pl.ds(0, 2), pl.ds(0, 31)], 2 + 4 * part)
+        for there in (0, 1, 2, 3, 7, 4, 6, 5)[4 * part : 4 * part + 4]:
+            pl.when(there != z)(lambda there=there: late_z(there))
+
+    late_ref[z_slot] = mid_b_ref[z % 2, z // 2]
 
     finish_recv(mid_a_ref.at[pl.ds(0, 7)], 1)
     plane_bulk(mid_a_ref, early_ref, 5)
@@ -299,9 +310,10 @@
     finish_recv(late_ref.at[pl.ds(0, 7)], 4)
     finish_send(zsum_ref.at[pl.ds(0, 7)], 0)
     finish_send(mid_a_ref.at[pl.ds(0, 7)], 1)
-    finish_send(mid_b_ref.at[:, pl.ds(0, 31)], 2)
+    finish_send(mid_b_ref.at[:, pl.ds(0, 2), pl.ds(0, 31)], 2)
+    finish_send(mid_b_ref.at[:, pl.ds(0, 2), pl.ds(0, 31)], 6)
     finish_send(psum_ref.at[pl.ds(0, 31)], 3)
-    finish_send(mid_b_ref.at[pl.ds(0, 7)], 4)
+    finish_send(late_ref.at[pl.ds(0, 7)], 4)
     finish_send(early_ref.at[:, pl.ds(0, 31)], 5)
 
 
@@ -367,13 +379,13 @@
             pltpu.VMEM((4, 256, 256), bf16),
             pltpu.VMEM((2, 2048, 128), f32),
             pltpu.VMEM((8, 32, 8, 128), f32),
-            pltpu.VMEM((8, 32, 8, 128), f32),
+            pltpu.VMEM((2, 4, 32, 8, 128), f32),
             pltpu.VMEM((8, 32, 8, 128), f32),
             pltpu.VMEM((8, 1, 128), f32),
             pltpu.VMEM((32, 1, 128), f32),
             pltpu.SemaphoreType.DMA((2, 8)),
-            pltpu.SemaphoreType.DMA((6,)),
-            pltpu.SemaphoreType.DMA((6,)),
+            pltpu.SemaphoreType.DMA((7,)),
+            pltpu.SemaphoreType.DMA((7,)),
             pltpu.SemaphoreType.REGULAR((2,)),
         ],
         compiler_params=pltpu.CompilerParams(

time: 56.3 us -> 55.8 us (level)
  the two profiles are of different devices: /device:TPU:64 before, /device:TPU:74 now
where the time goes in v7:
time: 55.8 us; the launch traced here: 55.7 us
  Pallas kernels  55.1 us (99%)
  between operations  0.64 us (1%)
    pallas_call x1, Pallas kernels, per_device(): pl.pallas_call(exchange_kernel, out_shape=(jax.ShapeDtypeStruct((2048, 12...  53.7 us
    pallas_call x1, Pallas kernels, per_device(): pl.pallas_call(place_kernel, out_shape=(jax.ShapeDtypeStruct((4096, 128),...  1.37 us

profile of v7, /device:TPU:74, one launch (start us, length us, event | category | flops | bytes accessed | tf_op | source)
XLA Modules:
  0.0 55.7 jit_solution(11938567861355747936)
XLA Ops:
  0.6 53.7 %shard_map.30 = (f32[2048,128]{1,0:T(8,128)S(1)}, f32[8,32,8,128]{3,2,1,0:T(8,128)S(1)}, f32[1,128]{1,0:T(1,128)S(1)}) custom-call(f32[256,2,8,128]{3,2,1,0:T(8,128)} %bitcast.12), custom_call_target="tpu_custom_call" | custom-call | tf_op jit(solution)/shard_map/pallas_call | solution.py:365
  54.4 1.4 %shard_map.31 = (f32[4096,128]{1,0:T(8,128)}, f32[3]{0:T(128)}) custom-call(f32[2048,128]{1,0:T(8,128)S(1)} %get-tuple-element.7.placed_ref, f32[2048,128]{1,0:T(8,128)S(1)} %bitcast.11, f32[1,128]{1,0:T(1,128)S(1)} %get-tuple-element.9.sums_ref), custom_call_target="tpu_custom_call" | custom-call | tf_op jit(solution)/shard_map/pallas_call | solution.py:395

commit v8 on v7

--- a/solution.py
+++ b/solution.py
@@ -100,16 +100,14 @@
     a_rows = a_ref.reshape(2 * SPAN, 128)
     zero = jnp.zeros((8, 128), jnp.float32)
 
-    def spread_half(half, squares):
+    def spread_half(half):
         for load in loads[half]:
             load.wait()
         if half == 0:
             for load in loads[1]:
                 load.start()
 
-        def spread(turn, carry):
-            squares, phase_real, phase_imag = carry
-            h = 15 - turn
+        def spread(h, _):
             middle = reverse_bits(h, 4)
             parts = [
                 [
@@ -118,13 +116,6 @@
                 ]
                 for b in range(2)
             ]
-            for b in (1, 0):
-                phase_real, phase_imag = (
-                    phase_real * cos_step + phase_imag * sin_step + parts[b][0],
-                    phase_imag * cos_step - phase_real * sin_step + parts[b][1],
-                )
-                for q in range(8):
-                    squares = squares + parts[b][q] * parts[b][q]
             v = [jnp.concatenate([parts[0][q], parts[1][q]], 0) for q in range(8)]
             real, imag = v[0::2], v[1::2]
             s02r, s02i = real[0] + real[2], imag[0] + imag[2]
@@ -148,9 +139,28 @@
                     low = (value - high.astype(jnp.float32)).astype(jnp.bfloat16)
                     bh_ref[g, rows, 128 * s : 128 * s + 128] = high
                     bl_ref[g, rows, 128 * s : 128 * s + 128] = low
+            return 0
+
+        lax.fori_loop(0, 16, spread, 0)
+
+    def sums_half(half, squares):
+        def add(turn, carry):
+            squares, phase_real, phase_imag = carry
+            middle = reverse_bits(15 - turn, 4)
+            for b in (1, 0):
+                part = [
+                    a_rows[pl.ds(half * SPAN + (middle + 16 * b) * 8 + q, 8, stride=PITCH), :]
+                    for q in range(8)
+                ]
+                phase_real, phase_imag = (
+                    phase_real * cos_step + phase_imag * sin_step + part[0],
+                    phase_imag * cos_step - phase_real * sin_step + part[1],
+                )
+                for q in range(8):
+                    squares = squares + part[q] * part[q]
             return squares, phase_real, phase_imag
 
-        return lax.fori_loop(0, 16, spread, (squares, zero, zero))
+        return lax.fori_loop(0, 16, add, (squares, zero, zero))
 
     def transform(half, first):
         for f in range(2):
@@ -185,7 +195,7 @@
     early_send = send_ref.reshape(2, 8, 32, 8, 128).at[0]
     late_send = send_ref.reshape(2, 2, 4, 32, 8, 128).at[1]
 
-    squares, phase_real_0, phase_imag_0 = spread_half(0, zero)
+    spread_half(0)
     def early_z(there):
         copy(z_peer(there), early_send.at[there % 2 * 4 + there // 2], mid_a_ref.at[z_slot], 1).start()
 
@@ -214,9 +224,11 @@
     def _():
         lax.fori_loop(1, 32, line_ready, 0)
 
-    squares, phase_real_1, phase_imag_1 = spread_half(1, squares)
+    spread_half(1)
     transform(1, 0)
     transform(1, 2)
+    squares, phase_real_0, phase_imag_0 = sums_half(0, zero)
+    squares, phase_real_1, phase_imag_1 = sums_half(1, squares)
 
     column = lax.broadcasted_iota(jnp.int32, (8, 128), 1)
     sub = lax.broadcasted_iota(jnp.int32, (8, 128), 0)

time: 55.8 us -> 55.8 us (level)
  the two profiles are of different devices: /device:TPU:74 before, /device:TPU:64 now
where the time goes in v8:
time: 55.8 us; the launch traced here: 55.7 us
  Pallas kernels  55 us (99%)
  between operations  0.64 us (1%)
    pallas_call x1, Pallas kernels, per_device(): pl.pallas_call(exchange_kernel, out_shape=(jax.ShapeDtypeStruct((2048, 12...  53.7 us
    pallas_call x1, Pallas kernels, per_device(): pl.pallas_call(place_kernel, out_shape=(jax.ShapeDtypeStruct((4096, 128),...  1.37 us

profile of v8, /device:TPU:64, one launch (start us, length us, event | category | flops | bytes accessed | tf_op | source)
XLA Modules:
  0.0 55.7 jit_solution(12662142692185642677)
XLA Ops:
  0.6 53.7 %shard_map.30 = (f32[2048,128]{1,0:T(8,128)S(1)}, f32[8,32,8,128]{3,2,1,0:T(8,128)S(1)}, f32[1,128]{1,0:T(1,128)S(1)}) custom-call(f32[256,2,8,128]{3,2,1,0:T(8,128)} %bitcast.12), custom_call_target="tpu_custom_call" | custom-call | tf_op jit(solution)/shard_map/pallas_call | solution.py:377
  54.3 1.4 %shard_map.31 = (f32[4096,128]{1,0:T(8,128)}, f32[3]{0:T(128)}) custom-call(f32[2048,128]{1,0:T(8,128)S(1)} %get-tuple-element.7.placed_ref, f32[2048,128]{1,0:T(8,128)S(1)} %bitcast.11, f32[1,128]{1,0:T(1,128)S(1)} %get-tuple-element.9.sums_ref), custom_call_target="tpu_custom_call" | custom-call | tf_op jit(solution)/shard_map/pallas_call | solution.py:407

commit v9 on v8

--- a/solution.py
+++ b/solution.py
@@ -46,8 +46,6 @@
         ]
         for half in range(2)
     ]
-    for load in loads[0]:
-        load.start()
 
     outer, inner = lax.axis_index("outer"), lax.axis_index("inner")
     y, c, x, z = outer // 2, outer % 2, inner // 8, inner % 8
@@ -65,8 +63,10 @@
         return (there_outer, there_x * 8 + z), there_outer * 4 + there_x
 
     barrier = pltpu.get_barrier_semaphore()
-    for d in range(1, 8):
+    for d in (4, 3, 5, 2, 6, 1, 7):
         pl.semaphore_signal(barrier, inc=1, device_id=z_peer((z + d) % 8), device_id_type=MESH)
+    for load in loads[0]:
+        load.start()
 
     def greet(t, _):
         pl.semaphore_signal(barrier, inc=1, device_id=plane_peer(t)[0], device_id_type=MESH)

time: 55.8 us -> 55.9 us (level)
  no operation moved by 1% of the time
where the time goes in v9:
time: 55.9 us; the launch traced here: 55.8 us
  Pallas kernels  55.2 us (99%)
  between operations  0.64 us (1%)
    pallas_call x1, Pallas kernels, per_device(): pl.pallas_call(exchange_kernel, out_shape=(jax.ShapeDtypeStruct((2048, 12...  53.8 us
    pallas_call x1, Pallas kernels, per_device(): pl.pallas_call(place_kernel, out_shape=(jax.ShapeDtypeStruct((4096, 128),...  1.37 us

profile of v9, /device:TPU:64, one launch (start us, length us, event | category | flops | bytes accessed | tf_op | source)
XLA Modules:
  0.0 55.8 jit_solution(6497496562900310526)
XLA Ops:
  0.6 53.8 %shard_map.30 = (f32[2048,128]{1,0:T(8,128)S(1)}, f32[8,32,8,128]{3,2,1,0:T(8,128)S(1)}, f32[1,128]{1,0:T(1,128)S(1)}) custom-call(f32[256,2,8,128]{3,2,1,0:T(8,128)} %bitcast.12), custom_call_target="tpu_custom_call" | custom-call | tf_op jit(solution)/shard_map/pallas_call | solution.py:377
  54.4 1.4 %shard_map.31 = (f32[4096,128]{1,0:T(8,128)}, f32[3]{0:T(128)}) custom-call(f32[2048,128]{1,0:T(8,128)S(1)} %get-tuple-element.7.placed_ref, f32[2048,128]{1,0:T(8,128)S(1)} %bitcast.11, f32[1,128]{1,0:T(1,128)S(1)} %get-tuple-element.9.sums_ref), custom_call_target="tpu_custom_call" | custom-call | tf_op jit(solution)/shard_map/pallas_call | solution.py:407
